TPU v7x, 32 devices: a whole 2x2x4 slice. The times are simulated.
32 devices in a mesh: dom: 8 (over y, x, core), orb: 4 (over z).
Axes of the slice: x: 2, y: 2, z: 4, core: 2. Of those that a mesh axis runs over, the one named last changes fastest.
Arguments:
- orbitals: float32 [8, 64, 64, 128], P('orb', 'dom'), may hold values from -10.8 to 10.8
- initial_guess: float32 [8, 64, 64, 128], P('orb', 'dom'), may hold values from -350 to 350
- potential: float32 [64, 64, 128], P('dom'), may hold values from 0.1 to 2
- perturbation: float32 [64, 64, 128], P('dom'), may hold values from -6 to 6
- level_shifts: float32 [8], replicated, may hold values from 0.05 to 2
- assignment: int32 [8], P('orb'), may hold values from 0 to 7, each once
Outputs:
- updated_response: float32 [8, 64, 64, 128], P('orb', 'dom')
Inputs may be any that keep to these rules, and one draw needn't show every extreme that they name: `assignment`: every energy index appears in exactly one slot.
All inputs are finite; a program needn't handle non-finite values.
Results may differ from a plain program's by a relative error of at most 0.0003.
Values sent between devices are 32-bit elements; how exact they have to be, the bound alone decides.
No kernel may reach another device: no remote copies, remote signals or barrier semaphores. Data moves between devices by JAX's collectives and lax.ppermute only.
A program may use at most 128 MiB of HBM per device.

v0:
```python
import functools

import jax
import jax.numpy as jnp
from jax import lax
from jax.experimental import pallas as pl
from jax.experimental.pallas import tpu as pltpu
from jax.sharding import PartitionSpec as P


OMEGA = 0.8
KINETIC = 8.0
LANES = 128
REACH = 3


F32 = jnp.float32
VMEM = pl.BlockSpec(memory_space=pltpu.VMEM)
SMEM = pl.BlockSpec(memory_space=pltpu.SMEM)
HBM = pl.BlockSpec(memory_space=pltpu.HBM)


def roll(x, shift, axis):
    return pltpu.roll(x, shift % x.shape[axis], axis)


def around(x, group):
    y, z = x.ndim - 2, x.ndim - 1
    total = roll(x, 1, y) + roll(x, -1, y)
    if group == x.shape[z]:
        return total + (roll(x, 1, z) + roll(x, -1, z))
    place = lax.broadcasted_iota(jnp.int32, x.shape, z) % group
    before = jnp.where(place == 0, roll(x, 1 - group, z), roll(x, 1, z))
    after = jnp.where(place == group - 1, roll(x, group - 1, z), roll(x, -1, z))
    return total + (before + after)


def exact_dot(values, table):
    high = values.astype(jnp.bfloat16)
    rest = values - high.astype(F32)
    middle = rest.astype(jnp.bfloat16)
    low = (rest - middle.astype(F32)).astype(jnp.bfloat16)
    dot = functools.partial(jnp.dot, preferred_element_type=F32)
    return dot(high, table) + (dot(middle, table) + dot(low, table))


def pair_table(rows, columns, value):
    r = lax.broadcasted_iota(jnp.int32, (rows, columns), 0)
    c = lax.broadcasted_iota(jnp.int32, (rows, columns), 1)
    return jnp.where(r // 2 == c, value, 0.0).astype(jnp.bfloat16)


def spread_table(rows, columns):
    r = lax.broadcasted_iota(jnp.int32, (rows, columns), 0)
    c = lax.broadcasted_iota(jnp.int32, (rows, columns), 1)
    return jnp.where(c // 2 == r, 1.0, 0.0).astype(jnp.bfloat16)


def load_all(pairs, sems):
    copies = [
        pltpu.make_async_copy(source, target, sems.at[k]) for k, (source, target) in enumerate(pairs)
    ]
    for copy in copies:
        copy.start()
    for copy in copies:
        copy.wait()


def own_source(i, x, constant, guess, orbital, potential, perturbation):
    value = guess[i, x]
    near = around(value, LANES)
    if x > 0:
        near = near + guess[i, x - 1]
    if x < guess.shape[1] - 1:
        near = near + guess[i, x + 1]
    return KINETIC * near - (constant + potential[x]) * value - perturbation[x] * orbital[i, x]


def edge_kernel(
    shifts_in, assigned_in, guess_in, orbital_in, potential_in, perturbation_in, up, down,
    shifts, assigned, guess, orbital, potential, perturbation, sems,
):
    fields = (guess, orbital, potential, perturbation)
    inputs = (shifts_in, assigned_in, guess_in, orbital_in, potential_in, perturbation_in)
    load_all(zip(inputs, (shifts, assigned) + fields), sems)
    count, depth = guess.shape[:2]
    for i in range(count):
        constant = 6.0 * KINETIC + shifts[assigned[i]]
        down[i] = guess[i, 0]
        up[i] = guess[i, depth - 1]
        for x in range(REACH):
            down[(1 + x) * count + i] = own_source(i, x, constant, *fields)
            up[(1 + x) * count + i] = own_source(i, depth - 1 - x, constant, *fields)
    for x in range(REACH):
        down[(1 + REACH) * count + x] = potential[x]
        up[(1 + REACH) * count + x] = potential[depth - 1 - x]


def own_kernel(
    shifts_in, assigned_in, guess_in, orbital_in, potential_in, perturbation_in, scaled, weight,
    shifts, assigned, guess, orbital, potential, perturbation, sems,
):
    fields = (guess, orbital, potential, perturbation)
    inputs = (shifts_in, assigned_in, guess_in, orbital_in, potential_in, perturbation_in)
    load_all(zip(inputs, (shifts, assigned) + fields), sems)
    count, depth = guess.shape[:2]
    for i in range(count):
        constant = 6.0 * KINETIC + shifts[assigned[i]]
        for x in range(depth):
            w = OMEGA / (constant + potential[x])
            weight[i, x] = KINETIC * w
            scaled[i, x] = w * own_source(i, x, constant, *fields)


def fine_kernel(
    shifts, assigned, own_scaled, own_weight, potential, low, high, up, down, estimate, scaled, weight, payload,
    all_scaled, all_weight, pairs,
):
    count, depth = own_scaled.shape[:2]
    planes = depth + 2 * REACH
    first = (1 + REACH) * count

    for i in range(count):
        constant = 6.0 * KINETIC + shifts[assigned[i]]
        for p in range(planes):
            x = p - REACH
            if 0 <= x < depth:
                kw = own_weight[i, x]
                g = own_scaled[i, x]
                if x == 0:
                    g = g + kw * low[i]
                if x == depth - 1:
                    g = g + kw * high[i]
            else:
                side, away = (low, -1 - x) if x < 0 else (high, x - depth)
                w = OMEGA / (constant + side[first + away])
                kw = KINETIC * w
                g = w * side[(1 + away) * count + i]
                if away == 0:
                    g = g + kw * (down if x < 0 else up)[i]
            all_weight[i, p] = kw
            all_scaled[i, p] = g
            if 2 <= p < planes - 2:
                scaled[i, p - 2] = g
                weight[i, p - 2] = kw
    for i in range(count):
        for p in range(1, planes - 1):
            g = all_scaled[i, p]
            near = around(g, LANES) + (all_scaled[i, p - 1] + all_scaled[i, p + 1])
            estimate[i, p - 1] = (2.0 - OMEGA) * g + all_weight[i, p] * near
    half = depth // 2
    for i in range(count):
        constant = 6.0 * KINETIC + shifts[assigned[i]]
        for q in range(half):
            total = None
            for x in (2 * q, 2 * q + 1):
                e = estimate[i, x + 2]
                near = around(e, LANES) + (estimate[i, x + 1] + estimate[i, x + 3])
                r = (constant + potential[x]) * (
                    (1.0 / OMEGA) * all_scaled[i, x + REACH] - e
                ) + KINETIC * near
                total = r if total is None else total + r
            pairs[q * count + i] = total
    for q in range(half):
        pairs[half * count + q] = potential[2 * q] + potential[2 * q + 1]
    rows = pairs.shape[1] // 2
    slots = pairs.shape[0] // 2
    even = pairs[:, pl.ds(0, rows, 2), :] + pairs[:, pl.ds(1, rows, 2), :]
    even = even.reshape(slots, 2, rows, LANES)
    both = jnp.concatenate([even[:, 0], even[:, 1]], axis=-1).reshape(slots * rows, 2 * LANES)
    payload[...] = exact_dot(both, pair_table(2 * LANES, LANES, 0.125)).reshape(slots, rows, LANES)


def coarse_kernel(
    place, shifts, assigned, gathered, estimate, scaled, weight, guess, update,
    scaled1, weight1, coef1, e1, pairs, spread2, a1, b1, spread1, a0, b0,
):
    members = gathered.shape[0]
    count, depth = guess.shape[:2]
    half = depth // 2
    reach = 3
    window = (2 * reach + 1) * half
    rows1 = gathered.shape[2]
    group1 = LANES // count
    k1 = KINETIC / 4
    k2 = KINETIC / 16

    def shift_lanes(group):
        lane = lax.broadcasted_iota(jnp.int32, (1, 1, LANES), 2) // group
        value = jnp.full((1, 1, LANES), shifts[assigned[0]], F32)
        for i in range(1, count):
            value = jnp.where(lane % count == i, shifts[assigned[i]], value)
        return value

    base1 = 6.0 * k1 + shift_lanes(group1)
    base2 = 6.0 * k2 + shift_lanes(group1 // 2)
    lane = lax.broadcasted_iota(jnp.int32, (1, rows1, LANES), 2)
    for s in range(2 * reach + 1):
        slot = lax.rem(place[0] + (s - reach + 2 * members), members)
        f = gathered[slot, 0:half]
        for t in range(half // 2):
            packed = gathered[slot, half + t : half + t + 1]
            swapped = roll(packed, LANES // 2, 2)
            coef1[s * half + 2 * t : s * half + 2 * t + 1] = jnp.where(
                lane < LANES // 2, packed, swapped
            )
            coef1[s * half + 2 * t + 1 : s * half + 2 * t + 2] = jnp.where(
                lane < LANES // 2, swapped, packed
            )
        w = OMEGA / (base1 + coef1[s * half : (s + 1) * half])
        weight1[s * half : (s + 1) * half] = k1 * w
        scaled1[s * half : (s + 1) * half] = w * f
    step = 4
    for p in range(1, window - 1, step):
        stop = min(p + step, window - 1)
        g = scaled1[p:stop]
        near = around(g, group1) + (scaled1[p - 1 : stop - 1] + scaled1[p + 1 : stop + 1])
        e1[p:stop] = (2.0 - OMEGA) * g + weight1[p:stop] * near
    coarse = window // 2 - 2
    for p in range(2, window - 2, step):
        stop = min(p + step, window - 2)
        e = e1[p:stop]
        near = around(e, group1) + (e1[p - 1 : stop - 1] + e1[p + 1 : stop + 1])
        c = coef1[p:stop]
        r = (base1 + c) * ((1.0 / OMEGA) * scaled1[p:stop] - e) + k1 * near
        for t in range(0, stop - p, 2):
            pairs[(p + t) // 2 - 1] = r[t] + r[t + 1]
            pairs[coarse + (p + t) // 2 - 1] = c[t] + c[t + 1]
    rows2 = rows1 // 2
    even = pairs[:, pl.ds(0, rows2, 2), :] + pairs[:, pl.ds(1, rows2, 2), :]
    both = exact_dot(
        even.reshape(2 * coarse * rows2, LANES), pair_table(LANES, LANES, 0.125)
    ).reshape(2 * coarse, rows2, LANES)
    w = OMEGA / (base2 + both[coarse:])
    g = w * both[:coarse]
    w = k2 * w
    e = None
    for _ in range(3):
        n = g.shape[0]
        if e is None:
            e = g
            mine = (2.0 - OMEGA) * g[1 : n - 1]
        else:
            mine = (1.0 - OMEGA) * e[1 : n - 1] + g[1 : n - 1]
        near = around(e[1 : n - 1], group1 // 2) + (e[0 : n - 2] + e[2:n])
        e = mine + w[1 : n - 1] * near
        g, w = g[1 : n - 1], w[1 : n - 1]
    n = e.shape[0]
    wide = exact_dot(e.reshape(n * rows2, LANES), spread_table(LANES, LANES))
    wide = wide.reshape(n, rows2, LANES)
    spread2[:, pl.ds(0, rows2, 2), :] = wide
    spread2[:, pl.ds(1, rows2, 2), :] = wide
    origin = reach * half
    for q in range(-3, half + 3):
        a1[q + 3] = e1[origin + q] + spread2[(q + 4) // 2]

    def sweep1(source, start, stop, offset):
        e = source[start - offset : stop - offset]
        near = around(e, group1) + (
            source[start - 1 - offset : stop - 1 - offset]
            + source[start + 1 - offset : stop + 1 - offset]
        )
        window = slice(origin + start, origin + stop)
        return (1.0 - OMEGA) * e + scaled1[window] + weight1[window] * near

    for q in range(-2, half + 2, 4):
        b1[q + 2 : q + 6] = sweep1(a1, q, q + 4, -3)
    last = sweep1(b1, -1, half + 1, -2)
    n = last.shape[0]
    wide = exact_dot(last.reshape(n * rows1, LANES), spread_table(LANES, count * LANES))
    wide = wide.reshape(n, rows1, count * LANES)
    for i in range(count):
        part = wide[:, :, i * LANES : (i + 1) * LANES]
        spread1[i, :, pl.ds(0, rows1, 2), :] = part
        spread1[i, :, pl.ds(1, rows1, 2), :] = part
    for i in range(count):
        for p in range(depth + 4):
            a0[i, p] = estimate[i, p] + spread1[i, p // 2]
    for i in range(count):
        for p in range(depth + 2):
            e = a0[i, p + 1]
            near = around(e, LANES) + (a0[i, p] + a0[i, p + 2])
            b0[i, p] = (1.0 - OMEGA) * e + scaled[i, p] + weight[i, p] * near
    for i in range(count):
        for p in range(depth):
            e = b0[i, p + 1]
            near = around(e, LANES) + (b0[i, p] + b0[i, p + 2])
            update[i, p] = guess[i, p] + (
                (1.0 - OMEGA) * e + scaled[i, p + 1] + weight[i, p + 1] * near
            )


def row_sums(blocks, update, out, first):
    count, depth, rows = update.shape[:3]

    def body(x, totals):
        totals = list(totals)
        u = [update[i, x].reshape(rows // 8, 8, LANES) for i in range(count)]
        for r, block in enumerate(blocks):
            for j in range(count):
                o = block(j, x).reshape(rows // 8, 8, LANES)
                for i in range(count):
                    totals[(r * count + j) * count + i] += jnp.sum(o * u[i], axis=0)
        return tuple(totals)

    zero = jnp.zeros((8, LANES), F32)
    totals = lax.fori_loop(0, depth, body, (zero,) * (len(blocks) * count * count))
    for k, total in enumerate(totals):
        out[first + k : first + k + 1] = jnp.sum(total, axis=0, keepdims=True)


def reader(*refs):
    def read(j, x):
        value = refs[0][j, x]
        for ref in refs[1:]:
            value = value + ref[j, x]
        return value

    return read


def early_kernel(blocks, update, own_in, *refs):
    others, (out, own, sem) = refs[:blocks], refs[blocks:]
    copy = pltpu.make_async_copy(own_in, own, sem)
    copy.start()
    copy.wait()
    row_sums([reader(own)] + [reader(other) for other in others], update, out, 0)


def late_kernel(update, early, *refs):
    last, out = refs[:-1], refs[-1]
    rows = early.shape[0]
    out[0:rows] = early[...]
    row_sums([reader(*last)], update, out, rows)


def project_kernel(blocks, parts, cells, update, own_in, *refs):
    others, last = refs[:blocks], refs[blocks:-3 - parts]
    sums, (out, own, sem) = refs[-3 - parts : -3], refs[-3:]
    copy = pltpu.make_async_copy(own_in, own, sem)
    copy.start()
    count, depth, _ = update.shape[:3]
    total = sums[0][...]
    for part in sums[1:]:
        total = total + part[...]
    overlap = jnp.sum(total, axis=1, keepdims=True) / cells
    copy.wait()
    reads = [reader(own)] + [reader(other) for other in others] + [reader(*last)]

    def body(x, carry):
        values = [update[i, x] for i in range(count)]
        for r, read in enumerate(reads):
            for j in range(count):
                o = read(j, x)
                for i in range(count):
                    k = (r * count + j) * count + i
                    values[i] = values[i] - overlap[k : k + 1] * o
        for i in range(count):
            out[i, x] = values[i]
        return carry

    lax.fori_loop(0, depth, body, 0)


def gather_blocks(block, axis):
    n = lax.axis_size(axis)
    if n == 4:
        first = lax.ppermute(block, axis, [(0, 2), (3, 1), (2, 3), (1, 0)])
        second = lax.ppermute(block, axis, [(1, 3), (2, 0), (0, 1), (3, 2)])
        inner = lax.ppermute(block, axis, [(1, 2), (2, 1)])
        outer = lax.ppermute(first, axis, [(2, 3), (1, 0)])
        return [first, second], [inner, outer]
    blocks = []
    for r in range(1, n):
        blocks.append(lax.ppermute(block, axis, [((i + r) % n, i) for i in range(n)]))
    return blocks[:-1], blocks[-1:]


def reduce_parts(value, axis):
    n = lax.axis_size(axis)
    if n & (n - 1):
        return [lax.psum(value, axis)]
    parts, stride, width = [value], 1, 2
    while stride < n:
        total = parts[0]
        for part in parts[1:]:
            total = total + part
        width = min(width, n // stride)
        parts = [total] + [
            lax.ppermute(total, axis, [(i, i ^ (k * stride)) for i in range(n)])
            for k in range(width - 1, 0, -1)
        ]
        stride, width = stride * width, 4
    return parts


def on_device(orbitals, initial_guess, potential, perturbation, level_shifts, assignment):
    count, depth, ny, nz = orbitals.shape
    near = lambda x: pltpu.with_memory_space_constraint(x, pltpu.HBM)
    members = lax.axis_size("dom")
    half, rows1 = depth // 2, ny // 2
    assert nz == LANES and count * (nz // 2) == LANES and depth >= 2 * REACH
    plane = (ny, nz)
    shape = lambda *dims: jax.ShapeDtypeStruct(dims, F32)
    scratch = lambda *dims: pltpu.VMEM(dims, F32)
    params = pltpu.CompilerParams(vmem_limit_bytes=24 * 1024 * 1024)
    place = lax.axis_index("dom").astype(jnp.int32).reshape(1)

    blocks, last = gather_blocks(orbitals, "orb")

    message = (1 + REACH) * count + REACH
    inputs = tuple(
        map(near, (level_shifts, assignment, initial_guess, orbitals, potential, perturbation))
    )
    local = [
        pltpu.SMEM(level_shifts.shape, F32),
        pltpu.SMEM(assignment.shape, jnp.int32),
        scratch(count, depth, *plane),
        scratch(count, depth, *plane),
        scratch(depth, *plane),
        scratch(depth, *plane),
        pltpu.SemaphoreType.DMA((6,)),
    ]
    up, down = pl.pallas_call(
        edge_kernel,
        out_shape=(shape(message, *plane),) * 2,
        in_specs=[HBM] * 6,
        out_specs=(VMEM,) * 2,
        scratch_shapes=local,
        compiler_params=params,
    )(*inputs)
    own_scaled, own_weight = pl.pallas_call(
        own_kernel,
        out_shape=(shape(count, depth, *plane),) * 2,
        in_specs=[HBM] * 6,
        out_specs=(VMEM,) * 2,
        scratch_shapes=local,
        compiler_params=params,
    )(*inputs)
    low = lax.ppermute(up, "dom", [(i, (i + 1) % members) for i in range(members)])
    high = lax.ppermute(down, "dom", [((i + 1) % members, i) for i in range(members)])

    estimate, scaled, weight, payload = pl.pallas_call(
        fine_kernel,
        out_shape=(
            shape(count, depth + 4, *plane),
            shape(count, depth + 2, *plane),
            shape(count, depth + 2, *plane),
            shape(half + half // 2, rows1, LANES),
        ),
        in_specs=[SMEM, SMEM] + [VMEM] * 7,
        out_specs=(VMEM,) * 4,
        scratch_shapes=[
            scratch(count, depth + 2 * REACH, *plane),
            scratch(count, depth + 2 * REACH, *plane),
            scratch(half * count + half, *plane),
        ],
        compiler_params=params,
    )(level_shifts, assignment, near(own_scaled), near(own_weight), potential, low, high, up, down)

    gathered = lax.all_gather(payload, "dom", axis=0)

    window = 7 * half
    update = pl.pallas_call(
        coarse_kernel,
        out_shape=shape(count, depth, *plane),
        in_specs=[SMEM, SMEM, SMEM] + [VMEM] * 5,
        out_specs=VMEM,
        scratch_shapes=[
            scratch(window, rows1, LANES),
            scratch(window, rows1, LANES),
            scratch(window, rows1, LANES),
            scratch(window, rows1, LANES),
            scratch(2 * (window // 2 - 2), rows1, LANES),
            scratch(6, rows1, LANES),
            scratch(half + 6, rows1, LANES),
            scratch(half + 4, rows1, LANES),
            scratch(count, half + 2, *plane),
            scratch(count, depth + 4, *plane),
            scratch(count, depth + 2, *plane),
        ],
        compiler_params=params,
    )(place, level_shifts, assignment, gathered, estimate, scaled, weight, initial_guess)

    own = [scratch(count, depth, *plane), pltpu.SemaphoreType.DMA(())]
    rows = (1 + len(blocks)) * count * count
    sums = pl.pallas_call(
        functools.partial(early_kernel, len(blocks)),
        out_shape=shape(rows, LANES),
        in_specs=[VMEM, HBM] + [VMEM] * len(blocks),
        out_specs=VMEM,
        scratch_shapes=own,
        compiler_params=params,
    )(update, orbitals, *blocks)
    sums = pl.pallas_call(
        late_kernel,
        out_shape=shape(rows + count * count, LANES),
        in_specs=[VMEM] * (2 + len(last)),
        out_specs=VMEM,
        compiler_params=params,
    )(update, sums, *last)
    parts = reduce_parts(sums, "dom")
    cells = float(depth * members * ny * nz)
    return pl.pallas_call(
        functools.partial(project_kernel, len(blocks), len(parts), cells),
        out_shape=shape(count, depth, *plane),
        in_specs=[VMEM, HBM] + [VMEM] * (len(blocks) + len(last) + len(parts)),
        out_specs=VMEM,
        scratch_shapes=own,
        compiler_params=params,
    )(update, orbitals, *blocks, *last, *parts)


def solution(mesh):
    in_specs = (
        P("orb", "dom", None, None),
        P("orb", "dom", None, None),
        P("dom", None, None),
        P("dom", None, None),
        P(),
        P("orb"),
    )
    return jax.shard_map(
        on_device,
        mesh=mesh,
        in_specs=in_specs,
        out_specs=P("orb", "dom", None, None),
        check_vma=False,
    )
```

profile of v0, /device:TPU:0, one launch (start us, length us, event | category | flops | bytes accessed | tf_op | source)
XLA Modules:
  0.0 49.1 jit_solution(4509684194149861962)
XLA Ops:
  0.0 4.1 %collective-permute-start.2 = (f32[2,8,64,128]{3,2,1,0:T(8,128)}, f32[2,8,64,128]{3,2,1,0:T(8,128)S(1)}, u32[]{:S(2)}, u32[]{:S(2)}) collective-permute-start(f32[2,8,64,128]{3,2,1,0:T(8,128)} %own_in.3), channel_id=1, source_target_pairs={{0,2},{3,1},{2,3},{1,0},{4,6},{7,5},{6,7},{5,4},{8,10},{11,9},{10,... | collective-permute-start | bytes 1572872 | tf_op jit(solution)/shard_map/ppermute | solution.py:368
  4.1 2.4 %shard_map.65 = (f32[11,64,128]{2,1,0:T(8,128)S(1)}, f32[11,64,128]{2,1,0:T(8,128)}) custom-call(f32[8]{0:T(128)} %shifts.3, s32[2]{0:T(128)} %assigned.3, f32[2,8,64,128]{3,2,1,0:T(8,128)} %guess.1, f32[2,8,64,128]{3,2,1,0:T(8,128)} %own_in.3, f32[8,64,128]{2,1,0:T(8,128)} %potential.1, f32[8,64,128]{2,1,0:T(8,128)} %perturbation_in.3), custom_call_target="tpu_custom_call" | custom-call | tf_op jit(solution)/shard_map/pallas_call | solution.py:424
  6.5 0.1 collective-permute-start
  6.5 0.0 copy-start.3
  6.5 2.6 %collective-permute-start.1 = (f32[11,64,128]{2,1,0:T(8,128)}, f32[11,64,128]{2,1,0:T(8,128)}, u32[]{:S(2)}, u32[]{:S(2)}) collective-permute-start(f32[11,64,128]{2,1,0:T(8,128)} %get-tuple-element.16.down), channel_id=1, source_target_pairs={{4,0},{8,4},{12,8},{16,12},{20,16},{24,20},{28,24},{0,28},{5,1},{9... | collective-permute-start | bytes 1081352 | tf_op jit(solution)/shard_map/ppermute | solution.py:441
  9.2 0.7 %collective-permute-start.4 = (f32[2,8,64,128]{3,2,1,0:T(8,128)S(1)}, f32[2,8,64,128]{3,2,1,0:T(8,128)S(1)}, u32[]{:S(2)}, u32[]{:S(2)}) collective-permute-start(f32[2,8,64,128]{3,2,1,0:T(8,128)S(1)} %copy-done), channel_id=1, source_target_pairs={{1,2},{2,1},{5,6},{6,5},{9,10},{10,9},{13,14},{14,13},{17,18},{18,... | collective-permute-start | bytes 1572872 | tf_op jit(solution)/shard_map/ppermute | solution.py:370
  9.9 6.9 %collective-permute-done.2.refs_0_ = f32[2,8,64,128]{3,2,1,0:T(8,128)S(1)} collective-permute-done((f32[2,8,64,128]{3,2,1,0:T(8,128)}, f32[2,8,64,128]{3,2,1,0:T(8,128)S(1)}, u32[]{:S(2)}, u32[]{:S(2)}) %collective-permute-start.2) | collective-permute-done | bytes 524320 | tf_op jit(solution)/shard_map/ppermute | solution.py:368
  16.7 1.3 %collective-permute-start.5 = (f32[2,8,64,128]{3,2,1,0:T(8,128)S(1)}, f32[2,8,64,128]{3,2,1,0:T(8,128)S(1)}, u32[]{:S(2)}, u32[]{:S(2)}) collective-permute-start(f32[2,8,64,128]{3,2,1,0:T(8,128)S(1)} %collective-permute-done.2.refs_0_), channel_id=1, source_target_pairs={{2,3},{1,0},{6,7},{5,4},{10,11},{9,8},{14,15},{13,12},{18,19},{17,... | collective-permute-start | bytes 1572872 | tf_op jit(solution)/shard_map/ppermute | solution.py:371
  18.0 1.8 %shard_map.64 = (f32[2,8,64,128]{3,2,1,0:T(8,128)S(1)}, f32[2,8,64,128]{3,2,1,0:T(8,128)S(1)}) custom-call(f32[8]{0:T(128)} %shifts.3, s32[2]{0:T(128)} %assigned.3, f32[2,8,64,128]{3,2,1,0:T(8,128)} %guess.1, f32[2,8,64,128]{3,2,1,0:T(8,128)} %own_in.3, f32[8,64,128]{2,1,0:T(8,128)} %potential.1, f32[8,64,128]{2,1,0:T(8,128)} %perturbation_in.3), custom_call_target="tpu_custom_call" | custom-call | tf_op jit(solution)/shard_map/pallas_call | solution.py:432
  19.8 0.0 copy-start.4
  19.8 0.8 %copy-done.4 = f32[2,8,64,128]{3,2,1,0:T(8,128)} copy-done((f32[2,8,64,128]{3,2,1,0:T(8,128)}, f32[2,8,64,128]{3,2,1,0:T(8,128)S(1)}, u32[]{:S(2)}) %copy-start.4) | copy-done | bytes 524312
  20.6 0.8 %copy-done.5 = f32[2,8,64,128]{3,2,1,0:T(8,128)} copy-done((f32[2,8,64,128]{3,2,1,0:T(8,128)}, f32[2,8,64,128]{3,2,1,0:T(8,128)S(1)}, u32[]{:S(2)}) %copy-start.5) | copy-done | bytes 524312
  21.4 0.0 collective-permute-done.1.high
  21.4 0.0 copy-start.7
  21.4 0.6 %copy-done.6 = f32[8]{0:T(128)S(1)} copy-done((f32[8]{0:T(128)S(1)}, f32[8]{0:T(128)}, u32[]{:S(2)}) %copy-start.6) | copy-done | bytes 56
  22.1 0.0 copy-done.7
  22.1 2.7 %shard_map.66 = (f32[2,12,64,128]{3,2,1,0:T(8,128)S(1)}, f32[2,10,64,128]{3,2,1,0:T(8,128)S(1)}, f32[2,10,64,128]{3,2,1,0:T(8,128)S(1)}, f32[6,32,128]{2,1,0:T(8,128)S(1)}) custom-call(f32[8]{0:T(128)S(1)} %copy-done.6, s32[2]{0:T(128)S(1)} %copy-done.7, f32[2,8,64,128]{3,2,1,0:T(8,128)} %copy-done.4, f32[2,8,64,128]{3,2,1,0:T(8,128)} %copy-done.5, ...), custom_call_target="tpu_custom_call" | custom-call | tf_op jit(solution)/shard_map/pallas_call | solution.py:443
  24.8 0.0 copy-start.2
  24.8 10.5 %all-gather = f32[48,32,128]{2,1,0:T(8,128)S(1)} all-gather(f32[6,32,128]{2,1,0:T(8,128)S(1)} %get-tuple-element.17), channel_id=2, replica_groups=mesh['dom'=8,'orb'=4] {'dom'}, dimensions={0}, use_global_device_ids=true | all-gather | bytes 884736 | tf_op jit(solution)/shard_map/all_gather | solution.py:461
  35.4 3.8 %shard_map.67.update = f32[2,8,64,128]{3,2,1,0:T(8,128)S(1)} custom-call(s32[1]{0:T(128)} %bitcast.place, f32[8]{0:T(128)S(1)} %copy-done.6, s32[2]{0:T(128)S(1)} %copy-done.7, f32[8,6,32,128]{3,2,1,0:T(8,128)S(1)} %bitcast.2, f32[2,12,64,128]{3,2,1,0:T(8,128)S(1)} %get-tuple-element.18.estimate, f32[2,10,64,128]{3,2,1,0:T(8,128)S(1)} %get-tuple-element.19.scaled, ...), custom_call_target="tpu_custom_call" | custom-call | tf_op jit(solution)/shard_map/pallas_call | solution.py:464
  39.2 0.3 shard_map.68.early
  39.6 0.2 collective-permute-done.5.refs_1_.refs_3_
  39.8 0.2 shard_map.69
  39.9 0.3 collective-permute-start.6
  40.2 1.0 %collective-permute-done.6 = f32[16,128]{1,0:T(8,128)S(1)} collective-permute-done((f32[16,128]{1,0:T(8,128)S(1)}, f32[16,128]{1,0:T(8,128)S(1)}, u32[]{:S(2)}, u32[]{:S(2)}) %collective-permute-start.6) | collective-permute-done | bytes 8224 | tf_op jit(solution)/shard_map/ppermute | solution.py:390
  41.2 2.4 %collective-permute-start.7 = (f32[16,128]{1,0:T(8,128)S(1)}, f32[16,128]{1,0:T(8,128)S(1)}, u32[]{:S(2)}, u32[]{:S(2)}) collective-permute-start(f32[16,128]{1,0:T(8,128)S(1)} %add.3.refs_4_), channel_id=1, source_target_pairs={{0,24},{4,28},{8,16},{12,20},{16,8},{20,12},{24,0},{28,4},{1,25},{... | collective-permute-start | bytes 24584 | tf_op jit(solution)/shard_map/ppermute | solution.py:390
  43.6 0.5 %collective-permute-start.8 = (f32[16,128]{1,0:T(8,128)S(1)}, f32[16,128]{1,0:T(8,128)S(1)}, u32[]{:S(2)}, u32[]{:S(2)}) collective-permute-start(f32[16,128]{1,0:T(8,128)S(1)} %add.3.refs_4_), channel_id=1, source_target_pairs={{0,16},{4,20},{8,24},{12,28},{16,0},{20,4},{24,8},{28,12},{1,17},{... | collective-permute-start | bytes 24584 | tf_op jit(solution)/shard_map/ppermute | solution.py:390
  44.1 0.5 %collective-permute-start.9 = (f32[16,128]{1,0:T(8,128)S(1)}, f32[16,128]{1,0:T(8,128)S(1)}, u32[]{:S(2)}, u32[]{:S(2)}) collective-permute-start(f32[16,128]{1,0:T(8,128)S(1)} %add.3.refs_4_), channel_id=1, source_target_pairs={{0,8},{4,12},{8,0},{12,4},{16,24},{20,28},{24,16},{28,20},{1,9},{5... | collective-permute-start | bytes 24584 | tf_op jit(solution)/shard_map/ppermute | solution.py:390
  44.7 1.1 %collective-permute-done.7.refs_5_ = f32[16,128]{1,0:T(8,128)S(1)} collective-permute-done((f32[16,128]{1,0:T(8,128)S(1)}, f32[16,128]{1,0:T(8,128)S(1)}, u32[]{:S(2)}, u32[]{:S(2)}) %collective-permute-start.7) | collective-permute-done | bytes 8224 | tf_op jit(solution)/shard_map/ppermute | solution.py:390
  45.7 1.5 %collective-permute-done.8.refs_6_ = f32[16,128]{1,0:T(8,128)S(1)} collective-permute-done((f32[16,128]{1,0:T(8,128)S(1)}, f32[16,128]{1,0:T(8,128)S(1)}, u32[]{:S(2)}, u32[]{:S(2)}) %collective-permute-start.8) | collective-permute-done | bytes 8224 | tf_op jit(solution)/shard_map/ppermute | solution.py:390
  47.3 0.5 %collective-permute-done.9.refs_7_ = f32[16,128]{1,0:T(8,128)S(1)} collective-permute-done((f32[16,128]{1,0:T(8,128)S(1)}, f32[16,128]{1,0:T(8,128)S(1)}, u32[]{:S(2)}, u32[]{:S(2)}) %collective-permute-start.9) | collective-permute-done | bytes 8224 | tf_op jit(solution)/shard_map/ppermute | solution.py:390
  47.8 1.3 %shard_map.70 = f32[2,8,64,128]{3,2,1,0:T(8,128)} custom-call(f32[2,8,64,128]{3,2,1,0:T(8,128)S(1)} %shard_map.67.update, f32[2,8,64,128]{3,2,1,0:T(8,128)S(1)} %copy-done.1, f32[2,8,64,128]{3,2,1,0:T(8,128)S(1)} %collective-permute-done.2.refs_0_, f32[2,8,64,128]{3,2,1,0:T(8,128)S(1)} %collective-permute-done.3.refs_1_, ...), custom_call_target="tpu_custom_call" | custom-call | tf_op jit(solution)/shard_map/pallas_call | solution.py:504
  (13 shorter events, 0.0 us)
Async XLA Ops:
  0.0 9.2 %copy-start = (f32[2,8,64,128]{3,2,1,0:T(8,128)S(1)}, f32[2,8,64,128]{3,2,1,0:T(8,128)}, u32[]{:S(2)}) copy-start(f32[2,8,64,128]{3,2,1,0:T(8,128)} %own_in.3) | copy-start | bytes 1572868
  0.0 16.7 %collective-permute-start.2 = (f32[2,8,64,128]{3,2,1,0:T(8,128)}, f32[2,8,64,128]{3,2,1,0:T(8,128)S(1)}, u32[]{:S(2)}, u32[]{:S(2)}) collective-permute-start(f32[2,8,64,128]{3,2,1,0:T(8,128)} %own_in.3), channel_id=1, source_target_pairs={{0,2},{3,1},{2,3},{1,0},{4,6},{7,5},{6,7},{5,4},{8,10},{11,9},{10,... | collective-permute-start | bytes 1572872 | tf_op jit(solution)/shard_map/ppermute | solution.py:368
  6.5 14.9 %collective-permute-start = (f32[11,64,128]{2,1,0:T(8,128)S(1)}, f32[11,64,128]{2,1,0:T(8,128)}, u32[]{:S(2)}, u32[]{:S(2)}) collective-permute-start(f32[11,64,128]{2,1,0:T(8,128)S(1)} %get-tuple-element.15.up), channel_id=1, source_target_pairs={{0,4},{4,8},{8,12},{12,16},{16,20},{20,24},{24,28},{28,0},{1,5},{5... | collective-permute-start | bytes 1081352 | tf_op jit(solution)/shard_map/ppermute | solution.py:440
  6.5 14.9 %copy-start.3 = (f32[8,64,128]{2,1,0:T(8,128)S(1)}, f32[8,64,128]{2,1,0:T(8,128)}, u32[]{:S(2)}) copy-start(f32[8,64,128]{2,1,0:T(8,128)} %potential.1) | copy-start | bytes 786436
  6.5 14.9 %collective-permute-start.1 = (f32[11,64,128]{2,1,0:T(8,128)}, f32[11,64,128]{2,1,0:T(8,128)}, u32[]{:S(2)}, u32[]{:S(2)}) collective-permute-start(f32[11,64,128]{2,1,0:T(8,128)} %get-tuple-element.16.down), channel_id=1, source_target_pairs={{4,0},{8,4},{12,8},{16,12},{20,16},{24,20},{28,24},{0,28},{5,1},{9... | collective-permute-start | bytes 1081352 | tf_op jit(solution)/shard_map/ppermute | solution.py:441
  9.2 30.0 %collective-permute-start.3 = (f32[2,8,64,128]{3,2,1,0:T(8,128)S(1)}, f32[2,8,64,128]{3,2,1,0:T(8,128)S(1)}, u32[]{:S(2)}, u32[]{:S(2)}) collective-permute-start(f32[2,8,64,128]{3,2,1,0:T(8,128)S(1)} %copy-done), channel_id=1, source_target_pairs={{1,3},{2,0},{0,1},{3,2},{5,7},{6,4},{4,5},{7,6},{9,11},{10,8},{8,9... | collective-permute-start | bytes 1572872 | tf_op jit(solution)/shard_map/ppermute | solution.py:369
  9.2 30.4 %collective-permute-start.4 = (f32[2,8,64,128]{3,2,1,0:T(8,128)S(1)}, f32[2,8,64,128]{3,2,1,0:T(8,128)S(1)}, u32[]{:S(2)}, u32[]{:S(2)}) collective-permute-start(f32[2,8,64,128]{3,2,1,0:T(8,128)S(1)} %copy-done), channel_id=1, source_target_pairs={{1,2},{2,1},{5,6},{6,5},{9,10},{10,9},{13,14},{14,13},{17,18},{18,... | collective-permute-start | bytes 1572872 | tf_op jit(solution)/shard_map/ppermute | solution.py:370
  16.7 23.0 %collective-permute-start.5 = (f32[2,8,64,128]{3,2,1,0:T(8,128)S(1)}, f32[2,8,64,128]{3,2,1,0:T(8,128)S(1)}, u32[]{:S(2)}, u32[]{:S(2)}) collective-permute-start(f32[2,8,64,128]{3,2,1,0:T(8,128)S(1)} %collective-permute-done.2.refs_0_), channel_id=1, source_target_pairs={{2,3},{1,0},{6,7},{5,4},{10,11},{9,8},{14,15},{13,12},{18,19},{17,... | collective-permute-start | bytes 1572872 | tf_op jit(solution)/shard_map/ppermute | solution.py:371
  19.8 0.8 %copy-start.4 = (f32[2,8,64,128]{3,2,1,0:T(8,128)}, f32[2,8,64,128]{3,2,1,0:T(8,128)S(1)}, u32[]{:S(2)}) copy-start(f32[2,8,64,128]{3,2,1,0:T(8,128)S(1)} %get-tuple-element.13.own_scaled) | copy-start | bytes 1572868
  20.6 0.8 %copy-start.5 = (f32[2,8,64,128]{3,2,1,0:T(8,128)}, f32[2,8,64,128]{3,2,1,0:T(8,128)S(1)}, u32[]{:S(2)}) copy-start(f32[2,8,64,128]{3,2,1,0:T(8,128)S(1)} %get-tuple-element.14.own_weight) | copy-start | bytes 1572868
  21.4 0.7 %copy-start.6 = (f32[8]{0:T(128)S(1)}, f32[8]{0:T(128)}, u32[]{:S(2)}) copy-start(f32[8]{0:T(128)} %shifts.3) | copy-start | bytes 100
  21.4 0.7 %copy-start.7 = (s32[2]{0:T(128)S(1)}, s32[2]{0:T(128)}, u32[]{:S(2)}) copy-start(s32[2]{0:T(128)} %assigned.3) | copy-start | bytes 28
  24.8 10.6 %copy-start.2 = (f32[2,8,64,128]{3,2,1,0:T(8,128)S(1)}, f32[2,8,64,128]{3,2,1,0:T(8,128)}, u32[]{:S(2)}) copy-start(f32[2,8,64,128]{3,2,1,0:T(8,128)} %guess.1) | copy-start | bytes 1572868
  35.4 3.9 %copy-start.1 = (f32[2,8,64,128]{3,2,1,0:T(8,128)S(1)}, f32[2,8,64,128]{3,2,1,0:T(8,128)}, u32[]{:S(2)}) copy-start(f32[2,8,64,128]{3,2,1,0:T(8,128)} %own_in.3) | copy-start | bytes 1572868
  39.9 1.2 %collective-permute-start.6 = (f32[16,128]{1,0:T(8,128)S(1)}, f32[16,128]{1,0:T(8,128)S(1)}, u32[]{:S(2)}, u32[]{:S(2)}) collective-permute-start(f32[16,128]{1,0:T(8,128)S(1)} %shard_map.69), channel_id=1, source_target_pairs={{0,4},{4,0},{8,12},{12,8},{16,20},{20,16},{24,28},{28,24},{1,5},{5... | collective-permute-start | bytes 24584 | tf_op jit(solution)/shard_map/ppermute | solution.py:390
  41.2 4.5 %collective-permute-start.7 = (f32[16,128]{1,0:T(8,128)S(1)}, f32[16,128]{1,0:T(8,128)S(1)}, u32[]{:S(2)}, u32[]{:S(2)}) collective-permute-start(f32[16,128]{1,0:T(8,128)S(1)} %add.3.refs_4_), channel_id=1, source_target_pairs={{0,24},{4,28},{8,16},{12,20},{16,8},{20,12},{24,0},{28,4},{1,25},{... | collective-permute-start | bytes 24584 | tf_op jit(solution)/shard_map/ppermute | solution.py:390
  43.6 3.7 %collective-permute-start.8 = (f32[16,128]{1,0:T(8,128)S(1)}, f32[16,128]{1,0:T(8,128)S(1)}, u32[]{:S(2)}, u32[]{:S(2)}) collective-permute-start(f32[16,128]{1,0:T(8,128)S(1)} %add.3.refs_4_), channel_id=1, source_target_pairs={{0,16},{4,20},{8,24},{12,28},{16,0},{20,4},{24,8},{28,12},{1,17},{... | collective-permute-start | bytes 24584 | tf_op jit(solution)/shard_map/ppermute | solution.py:390
  44.1 3.7 %collective-permute-start.9 = (f32[16,128]{1,0:T(8,128)S(1)}, f32[16,128]{1,0:T(8,128)S(1)}, u32[]{:S(2)}, u32[]{:S(2)}) collective-permute-start(f32[16,128]{1,0:T(8,128)S(1)} %add.3.refs_4_), channel_id=1, source_target_pairs={{0,8},{4,12},{8,0},{12,4},{16,24},{20,28},{24,16},{28,20},{1,9},{5... | collective-permute-start | bytes 24584 | tf_op jit(solution)/shard_map/ppermute | solution.py:390
where the time goes:
time: 49.4 us; the launch traced here: 49.1 us
  Pallas kernels  12.6 us (26%)
  starting transfers between devices  12.5 us (25%)
  waiting for transfers between devices  11.1 us (22%)
  blocking collectives  10.5 us (21%)
  local copies, waits for them, and re-layouts  2.25 us (5%)
    all_gather x1, blocking collectives, on_device(): gathered = lax.all_gather(payload, 'dom', axis=0)  10.5 us
    ppermute x1, waiting for transfers between devices, gather_blocks(): first = lax.ppermute(block, axis, [(0, 2), (3, 1), (2, 3), (1, 0)])  6.88 us
    ppermute x4, waiting for transfers between devices, reduce_parts(): lax.ppermute(total, axis, [(i, i ^ k * stride) for i in range(n)])  4.07 us
    ppermute x1, starting transfers between devices, gather_blocks(): first = lax.ppermute(block, axis, [(0, 2), (3, 1), (2, 3), (1, 0)])  4.06 us
    pallas_call x1, Pallas kernels, on_device(): pl.pallas_call(coarse_kernel, out_shape=shape(count, depth, *plane), in_s...  3.85 us
    ppermute x4, starting transfers between devices, reduce_parts(): lax.ppermute(total, axis, [(i, i ^ k * stride) for i in range(n)])  3.77 us
    pallas_call x1, Pallas kernels, on_device(): pl.pallas_call(fine_kernel, out_shape=(shape(count, depth + 4, *plane), s...  2.7 us
    ppermute x1, starting transfers between devices, on_device(): lax.ppermute(down, 'dom', [((i + 1) % members, i) for i in range(members)])  2.62 us
  transfers between devices with their start and end apart: 10, of which 6 were waited for; matrix products, arithmetic and copies ran while one was open for 0% of the time, Pallas kernels for 23%

commit v1 on v0

--- a/solution.py
+++ b/solution.py
@@ -319,12 +319,8 @@
     return read
 
 
-def early_kernel(blocks, update, own_in, *refs):
-    others, (out, own, sem) = refs[:blocks], refs[blocks:]
-    copy = pltpu.make_async_copy(own_in, own, sem)
-    copy.start()
-    copy.wait()
-    row_sums([reader(own)] + [reader(other) for other in others], update, out, 0)
+def early_kernel(update, own, *refs):
+    row_sums([reader(ref) for ref in (own,) + refs[:-1]], update, refs[-1], 0)
 
 
 def late_kernel(update, early, *refs):
@@ -334,20 +330,20 @@
     row_sums([reader(*last)], update, out, rows)
 
 
-def project_kernel(blocks, parts, cells, update, own_in, *refs):
-    others, last = refs[:blocks], refs[blocks:-3 - parts]
-    sums, (out, own, sem) = refs[-3 - parts : -3], refs[-3:]
-    copy = pltpu.make_async_copy(own_in, own, sem)
-    copy.start()
+def project_kernel(blocks, parts, cells, update, own, *refs):
+    others, last = refs[:blocks], refs[blocks : -3 - parts]
+    sums, (out_ref, out, sems) = refs[-3 - parts : -3], refs[-3:]
     count, depth, _ = update.shape[:3]
     total = sums[0][...]
     for part in sums[1:]:
         total = total + part[...]
     overlap = jnp.sum(total, axis=1, keepdims=True) / cells
-    copy.wait()
-    reads = [reader(own)] + [reader(other) for other in others] + [reader(*last)]
-
-    def body(x, carry):
+    reads = [reader(ref) for ref in (own,) + others] + [reader(*last)]
+
+    def store(x):
+        return pltpu.make_async_copy(out.at[:, x], out_ref.at[:, x], sems.at[x])
+
+    for x in range(depth):
         values = [update[i, x] for i in range(count)]
         for r, read in enumerate(reads):
             for j in range(count):
@@ -357,9 +353,9 @@
                     values[i] = values[i] - overlap[k : k + 1] * o
         for i in range(count):
             out[i, x] = values[i]
-        return carry
-
-    lax.fori_loop(0, depth, body, 0)
+        store(x).start()
+    for x in range(depth):
+        store(x).wait()
 
 
 def gather_blocks(block, axis):
@@ -386,10 +382,10 @@
         for part in parts[1:]:
             total = total + part
         width = min(width, n // stride)
-        parts = [total] + [
-            lax.ppermute(total, axis, [(i, i ^ (k * stride)) for i in range(n)])
-            for k in range(width - 1, 0, -1)
-        ]
+        parts = [total]
+        for k in range(width - 1, 0, -1):
+            pairs = [(i, i ^ (k * stride)) for i in range(n)]
+            parts.append(lax.ppermute(total, axis, pairs))
         stride, width = stride * width, 4
     return parts
 
@@ -482,14 +478,12 @@
         compiler_params=params,
     )(place, level_shifts, assignment, gathered, estimate, scaled, weight, initial_guess)
 
-    own = [scratch(count, depth, *plane), pltpu.SemaphoreType.DMA(())]
     rows = (1 + len(blocks)) * count * count
     sums = pl.pallas_call(
-        functools.partial(early_kernel, len(blocks)),
+        early_kernel,
         out_shape=shape(rows, LANES),
-        in_specs=[VMEM, HBM] + [VMEM] * len(blocks),
+        in_specs=[VMEM] * (2 + len(blocks)),
         out_specs=VMEM,
-        scratch_shapes=own,
         compiler_params=params,
     )(update, orbitals, *blocks)
     sums = pl.pallas_call(
@@ -504,9 +498,9 @@
     return pl.pallas_call(
         functools.partial(project_kernel, len(blocks), len(parts), cells),
         out_shape=shape(count, depth, *plane),
-        in_specs=[VMEM, HBM] + [VMEM] * (len(blocks) + len(last) + len(parts)),
-        out_specs=VMEM,
-        scratch_shapes=own,
+        in_specs=[VMEM] * (2 + len(blocks) + len(last) + len(parts)),
+        out_specs=HBM,
+        scratch_shapes=[scratch(count, depth, *plane), pltpu.SemaphoreType.DMA((depth,))],
         compiler_params=params,
     )(update, orbitals, *blocks, *last, *parts)
 

time: 49.4 us -> 49.1 us (level)
  no operation moved by 1% of the time
where the time goes in v1:
time: 49.1 us; the launch traced here: 48.9 us
  starting transfers between devices  12.4 us (25%)
  Pallas kernels  12.3 us (25%)
  waiting for transfers between devices  11.2 us (23%)
  blocking collectives  10.5 us (21%)
  local copies, waits for them, and re-layouts  2.25 us (5%)
    all_gather x1, blocking collectives, on_device(): gathered = lax.all_gather(payload, 'dom', axis=0)  10.5 us
    ppermute x1, waiting for transfers between devices, gather_blocks(): first = lax.ppermute(block, axis, [(0, 2), (3, 1), (2, 3), (1, 0)])  6.88 us
    ppermute x4, waiting for transfers between devices, reduce_parts(): parts.append(lax.ppermute(total, axis, pairs))  4.12 us
    ppermute x1, starting transfers between devices, gather_blocks(): first = lax.ppermute(block, axis, [(0, 2), (3, 1), (2, 3), (1, 0)])  4.06 us
    pallas_call x1, Pallas kernels, on_device(): pl.pallas_call(coarse_kernel, out_shape=shape(count, depth, *plane), in_s...  3.85 us
    ppermute x4, starting transfers between devices, reduce_parts(): parts.append(lax.ppermute(total, axis, pairs))  3.72 us
    pallas_call x1, Pallas kernels, on_device(): pl.pallas_call(fine_kernel, out_shape=(shape(count, depth + 4, *plane), s...  2.7 us
    ppermute x1, starting transfers between devices, on_device(): lax.ppermute(down, 'dom', [((i + 1) % members, i) for i in range(members)])  2.62 us
  transfers between devices with their start and end apart: 10, of which 6 were waited for; matrix products, arithmetic and copies ran while one was open for 0% of the time, Pallas kernels for 23%

profile of v1, /device:TPU:0, one launch (start us, length us, event | category | flops | bytes accessed | tf_op | source)
XLA Modules:
  0.0 48.9 jit_solution(9828185406327539775)
XLA Ops:
  0.0 4.1 %collective-permute-start.2 = (f32[2,8,64,128]{3,2,1,0:T(8,128)}, f32[2,8,64,128]{3,2,1,0:T(8,128)S(1)}, u32[]{:S(2)}, u32[]{:S(2)}) collective-permute-start(f32[2,8,64,128]{3,2,1,0:T(8,128)} %own.3), channel_id=1, source_target_pairs={{0,2},{3,1},{2,3},{1,0},{4,6},{7,5},{6,7},{5,4},{8,10},{11,9},{10,... | collective-permute-start | bytes 1572872 | tf_op jit(solution)/shard_map/ppermute | solution.py:364
  4.1 2.4 %shard_map.65 = (f32[11,64,128]{2,1,0:T(8,128)S(1)}, f32[11,64,128]{2,1,0:T(8,128)}) custom-call(f32[8]{0:T(128)} %shifts.3, s32[2]{0:T(128)} %assigned.3, f32[2,8,64,128]{3,2,1,0:T(8,128)} %guess.1, f32[2,8,64,128]{3,2,1,0:T(8,128)} %own.3, f32[8,64,128]{2,1,0:T(8,128)} %potential.1, f32[8,64,128]{2,1,0:T(8,128)} %perturbation_in.3), custom_call_target="tpu_custom_call" | custom-call | tf_op jit(solution)/shard_map/pallas_call | solution.py:420
  6.5 0.1 collective-permute-start
  6.5 0.0 copy-start.3
  6.5 2.6 %collective-permute-start.1 = (f32[11,64,128]{2,1,0:T(8,128)}, f32[11,64,128]{2,1,0:T(8,128)}, u32[]{:S(2)}, u32[]{:S(2)}) collective-permute-start(f32[11,64,128]{2,1,0:T(8,128)} %get-tuple-element.16.down), channel_id=1, source_target_pairs={{4,0},{8,4},{12,8},{16,12},{20,16},{24,20},{28,24},{0,28},{5,1},{9... | collective-permute-start | bytes 1081352 | tf_op jit(solution)/shard_map/ppermute | solution.py:437
  9.2 0.7 %collective-permute-start.4 = (f32[2,8,64,128]{3,2,1,0:T(8,128)S(1)}, f32[2,8,64,128]{3,2,1,0:T(8,128)S(1)}, u32[]{:S(2)}, u32[]{:S(2)}) collective-permute-start(f32[2,8,64,128]{3,2,1,0:T(8,128)S(1)} %copy-done), channel_id=1, source_target_pairs={{1,2},{2,1},{5,6},{6,5},{9,10},{10,9},{13,14},{14,13},{17,18},{18,... | collective-permute-start | bytes 1572872 | tf_op jit(solution)/shard_map/ppermute | solution.py:366
  9.9 6.9 %collective-permute-done.2.refs_0_ = f32[2,8,64,128]{3,2,1,0:T(8,128)S(1)} collective-permute-done((f32[2,8,64,128]{3,2,1,0:T(8,128)}, f32[2,8,64,128]{3,2,1,0:T(8,128)S(1)}, u32[]{:S(2)}, u32[]{:S(2)}) %collective-permute-start.2) | collective-permute-done | bytes 524320 | tf_op jit(solution)/shard_map/ppermute | solution.py:364
  16.7 1.3 %collective-permute-start.5 = (f32[2,8,64,128]{3,2,1,0:T(8,128)S(1)}, f32[2,8,64,128]{3,2,1,0:T(8,128)S(1)}, u32[]{:S(2)}, u32[]{:S(2)}) collective-permute-start(f32[2,8,64,128]{3,2,1,0:T(8,128)S(1)} %collective-permute-done.2.refs_0_), channel_id=1, source_target_pairs={{2,3},{1,0},{6,7},{5,4},{10,11},{9,8},{14,15},{13,12},{18,19},{17,... | collective-permute-start | bytes 1572872 | tf_op jit(solution)/shard_map/ppermute | solution.py:367
  18.0 1.8 %shard_map.64 = (f32[2,8,64,128]{3,2,1,0:T(8,128)S(1)}, f32[2,8,64,128]{3,2,1,0:T(8,128)S(1)}) custom-call(f32[8]{0:T(128)} %shifts.3, s32[2]{0:T(128)} %assigned.3, f32[2,8,64,128]{3,2,1,0:T(8,128)} %guess.1, f32[2,8,64,128]{3,2,1,0:T(8,128)} %own.3, f32[8,64,128]{2,1,0:T(8,128)} %potential.1, f32[8,64,128]{2,1,0:T(8,128)} %perturbation_in.3), custom_call_target="tpu_custom_call" | custom-call | tf_op jit(solution)/shard_map/pallas_call | solution.py:428
  19.8 0.0 copy-start.4
  19.8 0.8 %copy-done.4 = f32[2,8,64,128]{3,2,1,0:T(8,128)} copy-done((f32[2,8,64,128]{3,2,1,0:T(8,128)}, f32[2,8,64,128]{3,2,1,0:T(8,128)S(1)}, u32[]{:S(2)}) %copy-start.4) | copy-done | bytes 524312
  20.6 0.8 %copy-done.5 = f32[2,8,64,128]{3,2,1,0:T(8,128)} copy-done((f32[2,8,64,128]{3,2,1,0:T(8,128)}, f32[2,8,64,128]{3,2,1,0:T(8,128)S(1)}, u32[]{:S(2)}) %copy-start.5) | copy-done | bytes 524312
  21.4 0.0 collective-permute-done.1.high
  21.4 0.0 copy-start.7
  21.4 0.6 %copy-done.6 = f32[8]{0:T(128)S(1)} copy-done((f32[8]{0:T(128)S(1)}, f32[8]{0:T(128)}, u32[]{:S(2)}) %copy-start.6) | copy-done | bytes 56
  22.1 0.0 copy-done.7
  22.1 2.7 %shard_map.66 = (f32[2,12,64,128]{3,2,1,0:T(8,128)S(1)}, f32[2,10,64,128]{3,2,1,0:T(8,128)S(1)}, f32[2,10,64,128]{3,2,1,0:T(8,128)S(1)}, f32[6,32,128]{2,1,0:T(8,128)S(1)}) custom-call(f32[8]{0:T(128)S(1)} %copy-done.6, s32[2]{0:T(128)S(1)} %copy-done.7, f32[2,8,64,128]{3,2,1,0:T(8,128)} %copy-done.4, f32[2,8,64,128]{3,2,1,0:T(8,128)} %copy-done.5, ...), custom_call_target="tpu_custom_call" | custom-call | tf_op jit(solution)/shard_map/pallas_call | solution.py:439
  24.8 0.0 copy-start.2
  24.8 10.5 %all-gather = f32[48,32,128]{2,1,0:T(8,128)S(1)} all-gather(f32[6,32,128]{2,1,0:T(8,128)S(1)} %get-tuple-element.17), channel_id=2, replica_groups=mesh['dom'=8,'orb'=4] {'dom'}, dimensions={0}, use_global_device_ids=true | all-gather | bytes 884736 | tf_op jit(solution)/shard_map/all_gather | solution.py:457
  35.4 3.8 %shard_map.67.update = f32[2,8,64,128]{3,2,1,0:T(8,128)S(1)} custom-call(s32[1]{0:T(128)} %bitcast.place, f32[8]{0:T(128)S(1)} %copy-done.6, s32[2]{0:T(128)S(1)} %copy-done.7, f32[8,6,32,128]{3,2,1,0:T(8,128)S(1)} %bitcast.2, f32[2,12,64,128]{3,2,1,0:T(8,128)S(1)} %get-tuple-element.18.estimate, f32[2,10,64,128]{3,2,1,0:T(8,128)S(1)} %get-tuple-element.19.scaled, ...), custom_call_target="tpu_custom_call" | custom-call | tf_op jit(solution)/shard_map/pallas_call | solution.py:460
  39.2 0.3 shard_map.68.early
  39.5 0.2 collective-permute-done.5.refs_1_.refs_3_
  39.8 0.2 shard_map.69
  39.9 0.2 collective-permute-start.6
  40.2 1.0 %collective-permute-done.6 = f32[16,128]{1,0:T(8,128)S(1)} collective-permute-done((f32[16,128]{1,0:T(8,128)S(1)}, f32[16,128]{1,0:T(8,128)S(1)}, u32[]{:S(2)}, u32[]{:S(2)}) %collective-permute-start.6) | collective-permute-done | bytes 8224 | tf_op jit(solution)/shard_map/ppermute | solution.py:388
  41.2 2.4 %collective-permute-start.7 = (f32[16,128]{1,0:T(8,128)S(1)}, f32[16,128]{1,0:T(8,128)S(1)}, u32[]{:S(2)}, u32[]{:S(2)}) collective-permute-start(f32[16,128]{1,0:T(8,128)S(1)} %add.3.refs_4_), channel_id=1, source_target_pairs={{0,24},{4,28},{8,16},{12,20},{16,8},{20,12},{24,0},{28,4},{1,25},{... | collective-permute-start | bytes 24584 | tf_op jit(solution)/shard_map/ppermute | solution.py:388
  43.6 0.5 %collective-permute-start.8 = (f32[16,128]{1,0:T(8,128)S(1)}, f32[16,128]{1,0:T(8,128)S(1)}, u32[]{:S(2)}, u32[]{:S(2)}) collective-permute-start(f32[16,128]{1,0:T(8,128)S(1)} %add.3.refs_4_), channel_id=1, source_target_pairs={{0,16},{4,20},{8,24},{12,28},{16,0},{20,4},{24,8},{28,12},{1,17},{... | collective-permute-start | bytes 24584 | tf_op jit(solution)/shard_map/ppermute | solution.py:388
  44.1 0.5 %collective-permute-start.9 = (f32[16,128]{1,0:T(8,128)S(1)}, f32[16,128]{1,0:T(8,128)S(1)}, u32[]{:S(2)}, u32[]{:S(2)}) collective-permute-start(f32[16,128]{1,0:T(8,128)S(1)} %add.3.refs_4_), channel_id=1, source_target_pairs={{0,8},{4,12},{8,0},{12,4},{16,24},{20,28},{24,16},{28,20},{1,9},{5... | collective-permute-start | bytes 24584 | tf_op jit(solution)/shard_map/ppermute | solution.py:388
  44.7 1.1 %collective-permute-done.7.refs_5_ = f32[16,128]{1,0:T(8,128)S(1)} collective-permute-done((f32[16,128]{1,0:T(8,128)S(1)}, f32[16,128]{1,0:T(8,128)S(1)}, u32[]{:S(2)}, u32[]{:S(2)}) %collective-permute-start.7) | collective-permute-done | bytes 8224 | tf_op jit(solution)/shard_map/ppermute | solution.py:388
  45.7 1.5 %collective-permute-done.8.refs_6_ = f32[16,128]{1,0:T(8,128)S(1)} collective-permute-done((f32[16,128]{1,0:T(8,128)S(1)}, f32[16,128]{1,0:T(8,128)S(1)}, u32[]{:S(2)}, u32[]{:S(2)}) %collective-permute-start.8) | collective-permute-done | bytes 8224 | tf_op jit(solution)/shard_map/ppermute | solution.py:388
  47.3 0.5 %collective-permute-done.9.refs_7_ = f32[16,128]{1,0:T(8,128)S(1)} collective-permute-done((f32[16,128]{1,0:T(8,128)S(1)}, f32[16,128]{1,0:T(8,128)S(1)}, u32[]{:S(2)}, u32[]{:S(2)}) %collective-permute-start.9) | collective-permute-done | bytes 8224 | tf_op jit(solution)/shard_map/ppermute | solution.py:388
  47.8 1.1 %shard_map.70 = f32[2,8,64,128]{3,2,1,0:T(8,128)} custom-call(f32[2,8,64,128]{3,2,1,0:T(8,128)S(1)} %shard_map.67.update, f32[2,8,64,128]{3,2,1,0:T(8,128)S(1)} %copy-done.1, f32[2,8,64,128]{3,2,1,0:T(8,128)S(1)} %collective-permute-done.2.refs_0_, f32[2,8,64,128]{3,2,1,0:T(8,128)S(1)} %collective-permute-done.3.refs_1_, ...), custom_call_target="tpu_custom_call" | custom-call | tf_op jit(solution)/shard_map/pallas_call | solution.py:498
  (13 shorter events, 0.0 us)
Async XLA Ops:
  0.0 9.2 %copy-start = (f32[2,8,64,128]{3,2,1,0:T(8,128)S(1)}, f32[2,8,64,128]{3,2,1,0:T(8,128)}, u32[]{:S(2)}) copy-start(f32[2,8,64,128]{3,2,1,0:T(8,128)} %own.3) | copy-start | bytes 1572868
  0.0 16.7 %collective-permute-start.2 = (f32[2,8,64,128]{3,2,1,0:T(8,128)}, f32[2,8,64,128]{3,2,1,0:T(8,128)S(1)}, u32[]{:S(2)}, u32[]{:S(2)}) collective-permute-start(f32[2,8,64,128]{3,2,1,0:T(8,128)} %own.3), channel_id=1, source_target_pairs={{0,2},{3,1},{2,3},{1,0},{4,6},{7,5},{6,7},{5,4},{8,10},{11,9},{10,... | collective-permute-start | bytes 1572872 | tf_op jit(solution)/shard_map/ppermute | solution.py:364
  6.5 14.9 %collective-permute-start = (f32[11,64,128]{2,1,0:T(8,128)S(1)}, f32[11,64,128]{2,1,0:T(8,128)}, u32[]{:S(2)}, u32[]{:S(2)}) collective-permute-start(f32[11,64,128]{2,1,0:T(8,128)S(1)} %get-tuple-element.15.up), channel_id=1, source_target_pairs={{0,4},{4,8},{8,12},{12,16},{16,20},{20,24},{24,28},{28,0},{1,5},{5... | collective-permute-start | bytes 1081352 | tf_op jit(solution)/shard_map/ppermute | solution.py:436
  6.5 14.9 %copy-start.3 = (f32[8,64,128]{2,1,0:T(8,128)S(1)}, f32[8,64,128]{2,1,0:T(8,128)}, u32[]{:S(2)}) copy-start(f32[8,64,128]{2,1,0:T(8,128)} %potential.1) | copy-start | bytes 786436
  6.5 14.9 %collective-permute-start.1 = (f32[11,64,128]{2,1,0:T(8,128)}, f32[11,64,128]{2,1,0:T(8,128)}, u32[]{:S(2)}, u32[]{:S(2)}) collective-permute-start(f32[11,64,128]{2,1,0:T(8,128)} %get-tuple-element.16.down), channel_id=1, source_target_pairs={{4,0},{8,4},{12,8},{16,12},{20,16},{24,20},{28,24},{0,28},{5,1},{9... | collective-permute-start | bytes 1081352 | tf_op jit(solution)/shard_map/ppermute | solution.py:437
  9.2 30.0 %collective-permute-start.3 = (f32[2,8,64,128]{3,2,1,0:T(8,128)S(1)}, f32[2,8,64,128]{3,2,1,0:T(8,128)S(1)}, u32[]{:S(2)}, u32[]{:S(2)}) collective-permute-start(f32[2,8,64,128]{3,2,1,0:T(8,128)S(1)} %copy-done), channel_id=1, source_target_pairs={{1,3},{2,0},{0,1},{3,2},{5,7},{6,4},{4,5},{7,6},{9,11},{10,8},{8,9... | collective-permute-start | bytes 1572872 | tf_op jit(solution)/shard_map/ppermute | solution.py:365
  9.2 30.4 %collective-permute-start.4 = (f32[2,8,64,128]{3,2,1,0:T(8,128)S(1)}, f32[2,8,64,128]{3,2,1,0:T(8,128)S(1)}, u32[]{:S(2)}, u32[]{:S(2)}) collective-permute-start(f32[2,8,64,128]{3,2,1,0:T(8,128)S(1)} %copy-done), channel_id=1, source_target_pairs={{1,2},{2,1},{5,6},{6,5},{9,10},{10,9},{13,14},{14,13},{17,18},{18,... | collective-permute-start | bytes 1572872 | tf_op jit(solution)/shard_map/ppermute | solution.py:366
  16.7 23.0 %collective-permute-start.5 = (f32[2,8,64,128]{3,2,1,0:T(8,128)S(1)}, f32[2,8,64,128]{3,2,1,0:T(8,128)S(1)}, u32[]{:S(2)}, u32[]{:S(2)}) collective-permute-start(f32[2,8,64,128]{3,2,1,0:T(8,128)S(1)} %collective-permute-done.2.refs_0_), channel_id=1, source_target_pairs={{2,3},{1,0},{6,7},{5,4},{10,11},{9,8},{14,15},{13,12},{18,19},{17,... | collective-permute-start | bytes 1572872 | tf_op jit(solution)/shard_map/ppermute | solution.py:367
  19.8 0.8 %copy-start.4 = (f32[2,8,64,128]{3,2,1,0:T(8,128)}, f32[2,8,64,128]{3,2,1,0:T(8,128)S(1)}, u32[]{:S(2)}) copy-start(f32[2,8,64,128]{3,2,1,0:T(8,128)S(1)} %get-tuple-element.13.own_scaled) | copy-start | bytes 1572868
  20.6 0.8 %copy-start.5 = (f32[2,8,64,128]{3,2,1,0:T(8,128)}, f32[2,8,64,128]{3,2,1,0:T(8,128)S(1)}, u32[]{:S(2)}) copy-start(f32[2,8,64,128]{3,2,1,0:T(8,128)S(1)} %get-tuple-element.14.own_weight) | copy-start | bytes 1572868
  21.4 0.7 %copy-start.6 = (f32[8]{0:T(128)S(1)}, f32[8]{0:T(128)}, u32[]{:S(2)}) copy-start(f32[8]{0:T(128)} %shifts.3) | copy-start | bytes 100
  21.4 0.7 %copy-start.7 = (s32[2]{0:T(128)S(1)}, s32[2]{0:T(128)}, u32[]{:S(2)}) copy-start(s32[2]{0:T(128)} %assigned.3) | copy-start | bytes 28
  24.8 10.6 %copy-start.2 = (f32[2,8,64,128]{3,2,1,0:T(8,128)S(1)}, f32[2,8,64,128]{3,2,1,0:T(8,128)}, u32[]{:S(2)}) copy-start(f32[2,8,64,128]{3,2,1,0:T(8,128)} %guess.1) | copy-start | bytes 1572868
  35.4 3.9 %copy-start.1 = (f32[2,8,64,128]{3,2,1,0:T(8,128)S(1)}, f32[2,8,64,128]{3,2,1,0:T(8,128)}, u32[]{:S(2)}) copy-start(f32[2,8,64,128]{3,2,1,0:T(8,128)} %own.3) | copy-start | bytes 1572868
  39.9 1.2 %collective-permute-start.6 = (f32[16,128]{1,0:T(8,128)S(1)}, f32[16,128]{1,0:T(8,128)S(1)}, u32[]{:S(2)}, u32[]{:S(2)}) collective-permute-start(f32[16,128]{1,0:T(8,128)S(1)} %shard_map.69), channel_id=1, source_target_pairs={{0,4},{4,0},{8,12},{12,8},{16,20},{20,16},{24,28},{28,24},{1,5},{5... | collective-permute-start | bytes 24584 | tf_op jit(solution)/shard_map/ppermute | solution.py:388
  41.2 4.5 %collective-permute-start.7 = (f32[16,128]{1,0:T(8,128)S(1)}, f32[16,128]{1,0:T(8,128)S(1)}, u32[]{:S(2)}, u32[]{:S(2)}) collective-permute-start(f32[16,128]{1,0:T(8,128)S(1)} %add.3.refs_4_), channel_id=1, source_target_pairs={{0,24},{4,28},{8,16},{12,20},{16,8},{20,12},{24,0},{28,4},{1,25},{... | collective-permute-start | bytes 24584 | tf_op jit(solution)/shard_map/ppermute | solution.py:388
  43.6 3.7 %collective-permute-start.8 = (f32[16,128]{1,0:T(8,128)S(1)}, f32[16,128]{1,0:T(8,128)S(1)}, u32[]{:S(2)}, u32[]{:S(2)}) collective-permute-start(f32[16,128]{1,0:T(8,128)S(1)} %add.3.refs_4_), channel_id=1, source_target_pairs={{0,16},{4,20},{8,24},{12,28},{16,0},{20,4},{24,8},{28,12},{1,17},{... | collective-permute-start | bytes 24584 | tf_op jit(solution)/shard_map/ppermute | solution.py:388
  44.1 3.7 %collective-permute-start.9 = (f32[16,128]{1,0:T(8,128)S(1)}, f32[16,128]{1,0:T(8,128)S(1)}, u32[]{:S(2)}, u32[]{:S(2)}) collective-permute-start(f32[16,128]{1,0:T(8,128)S(1)} %add.3.refs_4_), channel_id=1, source_target_pairs={{0,8},{4,12},{8,0},{12,4},{16,24},{20,28},{24,16},{28,20},{1,9},{5... | collective-permute-start | bytes 24584 | tf_op jit(solution)/shard_map/ppermute | solution.py:388

commit v2 on v1

--- a/solution.py
+++ b/solution.py
@@ -309,28 +309,31 @@
         out[first + k : first + k + 1] = jnp.sum(total, axis=0, keepdims=True)
 
 
-def reader(*refs):
+def reader(ref, other=None, use_other=None):
     def read(j, x):
-        value = refs[0][j, x]
-        for ref in refs[1:]:
-            value = value + ref[j, x]
-        return value
+        if other is None:
+            return ref[j, x]
+        return jnp.where(use_other, other[j, x], ref[j, x])
 
     return read
+
+
+def chosen(last, outside):
+    return (outside[0] == 1,) if len(last) == 2 else ()
 
 
 def early_kernel(update, own, *refs):
     row_sums([reader(ref) for ref in (own,) + refs[:-1]], update, refs[-1], 0)
 
 
-def late_kernel(update, early, *refs):
+def late_kernel(outside, update, early, *refs):
     last, out = refs[:-1], refs[-1]
     rows = early.shape[0]
     out[0:rows] = early[...]
-    row_sums([reader(*last)], update, out, rows)
-
-
-def project_kernel(blocks, parts, cells, update, own, *refs):
+    row_sums([reader(*last, *chosen(last, outside))], update, out, rows)
+
+
+def project_kernel(blocks, parts, cells, outside, update, own, *refs):
     others, last = refs[:blocks], refs[blocks : -3 - parts]
     sums, (out_ref, out, sems) = refs[-3 - parts : -3], refs[-3:]
     count, depth, _ = update.shape[:3]
@@ -338,7 +341,7 @@
     for part in sums[1:]:
         total = total + part[...]
     overlap = jnp.sum(total, axis=1, keepdims=True) / cells
-    reads = [reader(ref) for ref in (own,) + others] + [reader(*last)]
+    reads = [reader(ref) for ref in (own,) + others] + [reader(*last, *chosen(last, outside))]
 
     def store(x):
         return pltpu.make_async_copy(out.at[:, x], out_ref.at[:, x], sems.at[x])
@@ -363,8 +366,8 @@
     if n == 4:
         first = lax.ppermute(block, axis, [(0, 2), (3, 1), (2, 3), (1, 0)])
         second = lax.ppermute(block, axis, [(1, 3), (2, 0), (0, 1), (3, 2)])
-        inner = lax.ppermute(block, axis, [(1, 2), (2, 1)])
-        outer = lax.ppermute(first, axis, [(2, 3), (1, 0)])
+        inner = lax.ppermute(block, axis, [(1, 2), (2, 1), (0, 0), (3, 3)])
+        outer = lax.ppermute(first, axis, [(2, 3), (1, 0), (0, 1), (3, 2)])
         return [first, second], [inner, outer]
     blocks = []
     for r in range(1, n):
@@ -403,6 +406,8 @@
     place = lax.axis_index("dom").astype(jnp.int32).reshape(1)
 
     blocks, last = gather_blocks(orbitals, "orb")
+    rank = lax.axis_index("orb")
+    outside = jnp.logical_or(rank == 0, rank == lax.axis_size("orb") - 1).astype(jnp.int32).reshape(1)
 
     message = (1 + REACH) * count + REACH
     inputs = tuple(
@@ -489,20 +494,20 @@
     sums = pl.pallas_call(
         late_kernel,
         out_shape=shape(rows + count * count, LANES),
-        in_specs=[VMEM] * (2 + len(last)),
+        in_specs=[SMEM] + [VMEM] * (2 + len(last)),
         out_specs=VMEM,
         compiler_params=params,
-    )(update, sums, *last)
+    )(outside, update, sums, *last)
     parts = reduce_parts(sums, "dom")
     cells = float(depth * members * ny * nz)
     return pl.pallas_call(
         functools.partial(project_kernel, len(blocks), len(parts), cells),
         out_shape=shape(count, depth, *plane),
-        in_specs=[VMEM] * (2 + len(blocks) + len(last) + len(parts)),
+        in_specs=[SMEM] + [VMEM] * (2 + len(blocks) + len(last) + len(parts)),
         out_specs=HBM,
         scratch_shapes=[scratch(count, depth, *plane), pltpu.SemaphoreType.DMA((depth,))],
         compiler_params=params,
-    )(update, orbitals, *blocks, *last, *parts)
+    )(outside, update, orbitals, *blocks, *last, *parts)
 
 
 def solution(mesh):

time: 49.1 us -> 49.9 us (1.016)
  starting transfers between devices: 12.4 us -> 13.6 us
    ppermute x2, starting transfers between devices: 1.96 us -> 2.95 us  [the longest x1 2.26 us: gather_blocks(): outer = lax.ppermute(first, axis, [(2, 3), (1, 0), (0, 1), (3, 2)])]
  transfers between devices with their start and end apart: 10 -> 10, of which waited for: 6 -> 5; matrix products, arithmetic and copies ran while one was open for 0% -> 0% of each run, Pallas kernels for 23% -> 22%
where the time goes in v2:
time: 49.9 us; the launch traced here: 49.7 us
  starting transfers between devices  13.6 us (27%)
  Pallas kernels  12.3 us (25%)
  waiting for transfers between devices  10.8 us (22%)
  blocking collectives  10.5 us (21%)
  local copies, waits for them, and re-layouts  2.25 us (5%)
    all_gather x1, blocking collectives, on_device(): gathered = lax.all_gather(payload, 'dom', axis=0)  10.5 us
    ppermute x1, waiting for transfers between devices, gather_blocks(): first = lax.ppermute(block, axis, [(0, 2), (3, 1), (2, 3), (1, 0)])  6.88 us
    ppermute x1, starting transfers between devices, gather_blocks(): first = lax.ppermute(block, axis, [(0, 2), (3, 1), (2, 3), (1, 0)])  4.06 us
    ppermute x4, waiting for transfers between devices, reduce_parts(): parts.append(lax.ppermute(total, axis, pairs))  3.94 us
    ppermute x4, starting transfers between devices, reduce_parts(): parts.append(lax.ppermute(total, axis, pairs))  3.92 us
    pallas_call x1, Pallas kernels, on_device(): pl.pallas_call(coarse_kernel, out_shape=shape(count, depth, *plane), in_s...  3.85 us
    pallas_call x1, Pallas kernels, on_device(): pl.pallas_call(fine_kernel, out_shape=(shape(count, depth + 4, *plane), s...  2.7 us
    ppermute x1, starting transfers between devices, on_device(): lax.ppermute(down, 'dom', [((i + 1) % members, i) for i in range(members)])  2.62 us
  transfers between devices with their start and end apart: 10, of which 5 were waited for; matrix products, arithmetic and copies ran while one was open for 0% of the time, Pallas kernels for 22%

profile of v2, /device:TPU:0, one launch (start us, length us, event | category | flops | bytes accessed | tf_op | source)
XLA Modules:
  0.0 49.7 jit_solution(16101827076228144103)
XLA Ops:
  0.0 4.1 %collective-permute-start.2 = (f32[2,8,64,128]{3,2,1,0:T(8,128)}, f32[2,8,64,128]{3,2,1,0:T(8,128)S(1)}, u32[]{:S(2)}, u32[]{:S(2)}) collective-permute-start(f32[2,8,64,128]{3,2,1,0:T(8,128)} %own.3), channel_id=1, source_target_pairs={{0,2},{3,1},{2,3},{1,0},{4,6},{7,5},{6,7},{5,4},{8,10},{11,9},{10,... | collective-permute-start | bytes 1572872 | tf_op jit(solution)/shard_map/ppermute | solution.py:367
  4.1 2.4 %shard_map.65 = (f32[11,64,128]{2,1,0:T(8,128)S(1)}, f32[11,64,128]{2,1,0:T(8,128)}) custom-call(f32[8]{0:T(128)} %shifts.3, s32[2]{0:T(128)} %assigned.3, f32[2,8,64,128]{3,2,1,0:T(8,128)} %guess.1, f32[2,8,64,128]{3,2,1,0:T(8,128)} %own.3, f32[8,64,128]{2,1,0:T(8,128)} %potential.1, f32[8,64,128]{2,1,0:T(8,128)} %perturbation_in.3), custom_call_target="tpu_custom_call" | custom-call | tf_op jit(solution)/shard_map/pallas_call | solution.py:425
  6.5 0.1 collective-permute-start
  6.5 0.0 copy-start.3
  6.5 2.6 %collective-permute-start.1 = (f32[11,64,128]{2,1,0:T(8,128)}, f32[11,64,128]{2,1,0:T(8,128)}, u32[]{:S(2)}, u32[]{:S(2)}) collective-permute-start(f32[11,64,128]{2,1,0:T(8,128)} %get-tuple-element.16.down), channel_id=1, source_target_pairs={{4,0},{8,4},{12,8},{16,12},{20,16},{24,20},{28,24},{0,28},{5,1},{9... | collective-permute-start | bytes 1081352 | tf_op jit(solution)/shard_map/ppermute | solution.py:442
  9.2 0.7 %collective-permute-start.4 = (f32[2,8,64,128]{3,2,1,0:T(8,128)S(1)}, f32[2,8,64,128]{3,2,1,0:T(8,128)S(1)}, u32[]{:S(2)}, u32[]{:S(2)}) collective-permute-start(f32[2,8,64,128]{3,2,1,0:T(8,128)S(1)} %copy-done), channel_id=1, source_target_pairs={{1,2},{2,1},{0,0},{3,3},{5,6},{6,5},{4,4},{7,7},{9,10},{10,9},{8,8... | collective-permute-start | bytes 1572872 | tf_op jit(solution)/shard_map/ppermute | solution.py:369
  9.9 6.9 %collective-permute-done.2.refs_0_ = f32[2,8,64,128]{3,2,1,0:T(8,128)S(1)} collective-permute-done((f32[2,8,64,128]{3,2,1,0:T(8,128)}, f32[2,8,64,128]{3,2,1,0:T(8,128)S(1)}, u32[]{:S(2)}, u32[]{:S(2)}) %collective-permute-start.2) | collective-permute-done | bytes 524320 | tf_op jit(solution)/shard_map/ppermute | solution.py:367
  16.7 2.3 %collective-permute-start.5 = (f32[2,8,64,128]{3,2,1,0:T(8,128)S(1)}, f32[2,8,64,128]{3,2,1,0:T(8,128)S(1)}, u32[]{:S(2)}, u32[]{:S(2)}) collective-permute-start(f32[2,8,64,128]{3,2,1,0:T(8,128)S(1)} %collective-permute-done.2.refs_0_), channel_id=1, source_target_pairs={{2,3},{1,0},{0,1},{3,2},{6,7},{5,4},{4,5},{7,6},{10,11},{9,8},{8,9... | collective-permute-start | bytes 1572872 | tf_op jit(solution)/shard_map/ppermute | solution.py:370
  19.0 1.8 %shard_map.64 = (f32[2,8,64,128]{3,2,1,0:T(8,128)S(1)}, f32[2,8,64,128]{3,2,1,0:T(8,128)S(1)}) custom-call(f32[8]{0:T(128)} %shifts.3, s32[2]{0:T(128)} %assigned.3, f32[2,8,64,128]{3,2,1,0:T(8,128)} %guess.1, f32[2,8,64,128]{3,2,1,0:T(8,128)} %own.3, f32[8,64,128]{2,1,0:T(8,128)} %potential.1, f32[8,64,128]{2,1,0:T(8,128)} %perturbation_in.3), custom_call_target="tpu_custom_call" | custom-call | tf_op jit(solution)/shard_map/pallas_call | solution.py:433
  20.8 0.0 copy-start.4
  20.8 0.8 %copy-done.4 = f32[2,8,64,128]{3,2,1,0:T(8,128)} copy-done((f32[2,8,64,128]{3,2,1,0:T(8,128)}, f32[2,8,64,128]{3,2,1,0:T(8,128)S(1)}, u32[]{:S(2)}) %copy-start.4) | copy-done | bytes 524312
  21.6 0.8 %copy-done.5 = f32[2,8,64,128]{3,2,1,0:T(8,128)} copy-done((f32[2,8,64,128]{3,2,1,0:T(8,128)}, f32[2,8,64,128]{3,2,1,0:T(8,128)S(1)}, u32[]{:S(2)}) %copy-start.5) | copy-done | bytes 524312
  22.4 0.0 collective-permute-done.low
  22.4 0.0 copy-start.7
  22.4 0.6 %copy-done.6 = f32[8]{0:T(128)S(1)} copy-done((f32[8]{0:T(128)S(1)}, f32[8]{0:T(128)}, u32[]{:S(2)}) %copy-start.6) | copy-done | bytes 56
  23.0 0.0 copy-done.7
  23.1 2.7 %shard_map.66 = (f32[2,12,64,128]{3,2,1,0:T(8,128)S(1)}, f32[2,10,64,128]{3,2,1,0:T(8,128)S(1)}, f32[2,10,64,128]{3,2,1,0:T(8,128)S(1)}, f32[6,32,128]{2,1,0:T(8,128)S(1)}) custom-call(f32[8]{0:T(128)S(1)} %copy-done.6, s32[2]{0:T(128)S(1)} %copy-done.7, f32[2,8,64,128]{3,2,1,0:T(8,128)} %copy-done.4, f32[2,8,64,128]{3,2,1,0:T(8,128)} %copy-done.5, ...), custom_call_target="tpu_custom_call" | custom-call | tf_op jit(solution)/shard_map/pallas_call | solution.py:444
  25.8 0.0 copy-start.2
  25.8 10.5 %all-gather = f32[48,32,128]{2,1,0:T(8,128)S(1)} all-gather(f32[6,32,128]{2,1,0:T(8,128)S(1)} %get-tuple-element.17), channel_id=2, replica_groups=mesh['dom'=8,'orb'=4] {'dom'}, dimensions={0}, use_global_device_ids=true | all-gather | bytes 884736 | tf_op jit(solution)/shard_map/all_gather | solution.py:462
  36.3 3.8 %shard_map.67.update = f32[2,8,64,128]{3,2,1,0:T(8,128)S(1)} custom-call(s32[1]{0:T(128)} %bitcast.1.place, f32[8]{0:T(128)S(1)} %copy-done.6, s32[2]{0:T(128)S(1)} %copy-done.7, f32[8,6,32,128]{3,2,1,0:T(8,128)S(1)} %bitcast.3, f32[2,12,64,128]{3,2,1,0:T(8,128)S(1)} %get-tuple-element.18.estimate, f32[2,10,64,128]{3,2,1,0:T(8,128)S(1)} %get-tuple-element.19.scaled, ...), custom_call_target="tpu_custom_call" | custom-call | tf_op jit(solution)/shard_map/pallas_call | solution.py:465
  40.2 0.3 shard_map.68.early
  40.5 0.0 collective-permute-done.4.refs_0_.refs_2_
  40.5 0.2 shard_map.69
  40.7 0.4 collective-permute-start.6
  41.1 0.8 %collective-permute-done.6 = f32[16,128]{1,0:T(8,128)S(1)} collective-permute-done((f32[16,128]{1,0:T(8,128)S(1)}, f32[16,128]{1,0:T(8,128)S(1)}, u32[]{:S(2)}, u32[]{:S(2)}) %collective-permute-start.6) | collective-permute-done | bytes 8224 | tf_op jit(solution)/shard_map/ppermute | solution.py:391
  42.0 1.5 %collective-permute-start.7 = (f32[16,128]{1,0:T(8,128)S(1)}, f32[16,128]{1,0:T(8,128)S(1)}, u32[]{:S(2)}, u32[]{:S(2)}) collective-permute-start(f32[16,128]{1,0:T(8,128)S(1)} %add.3.refs_4_), channel_id=1, source_target_pairs={{0,24},{4,28},{8,16},{12,20},{16,8},{20,12},{24,0},{28,4},{1,25},{... | collective-permute-start | bytes 24584 | tf_op jit(solution)/shard_map/ppermute | solution.py:391
  43.4 1.5 %collective-permute-start.8 = (f32[16,128]{1,0:T(8,128)S(1)}, f32[16,128]{1,0:T(8,128)S(1)}, u32[]{:S(2)}, u32[]{:S(2)}) collective-permute-start(f32[16,128]{1,0:T(8,128)S(1)} %add.3.refs_4_), channel_id=1, source_target_pairs={{0,16},{4,20},{8,24},{12,28},{16,0},{20,4},{24,8},{28,12},{1,17},{... | collective-permute-start | bytes 24584 | tf_op jit(solution)/shard_map/ppermute | solution.py:391
  44.9 0.5 %collective-permute-start.9 = (f32[16,128]{1,0:T(8,128)S(1)}, f32[16,128]{1,0:T(8,128)S(1)}, u32[]{:S(2)}, u32[]{:S(2)}) collective-permute-start(f32[16,128]{1,0:T(8,128)S(1)} %add.3.refs_4_), channel_id=1, source_target_pairs={{0,8},{4,12},{8,0},{12,4},{16,24},{20,28},{24,16},{28,20},{1,9},{5... | collective-permute-start | bytes 24584 | tf_op jit(solution)/shard_map/ppermute | solution.py:391
  45.5 1.1 %collective-permute-done.7.refs_5_ = f32[16,128]{1,0:T(8,128)S(1)} collective-permute-done((f32[16,128]{1,0:T(8,128)S(1)}, f32[16,128]{1,0:T(8,128)S(1)}, u32[]{:S(2)}, u32[]{:S(2)}) %collective-permute-start.7) | collective-permute-done | bytes 8224 | tf_op jit(solution)/shard_map/ppermute | solution.py:391
  46.5 0.6 %collective-permute-done.8.refs_6_ = f32[16,128]{1,0:T(8,128)S(1)} collective-permute-done((f32[16,128]{1,0:T(8,128)S(1)}, f32[16,128]{1,0:T(8,128)S(1)}, u32[]{:S(2)}, u32[]{:S(2)}) %collective-permute-start.8) | collective-permute-done | bytes 8224 | tf_op jit(solution)/shard_map/ppermute | solution.py:391
  47.1 1.5 %collective-permute-done.9.refs_7_ = f32[16,128]{1,0:T(8,128)S(1)} collective-permute-done((f32[16,128]{1,0:T(8,128)S(1)}, f32[16,128]{1,0:T(8,128)S(1)}, u32[]{:S(2)}, u32[]{:S(2)}) %collective-permute-start.9) | collective-permute-done | bytes 8224 | tf_op jit(solution)/shard_map/ppermute | solution.py:391
  48.6 1.1 %shard_map.70 = f32[2,8,64,128]{3,2,1,0:T(8,128)} custom-call(s32[1]{0:T(128)} %bitcast.outside, f32[2,8,64,128]{3,2,1,0:T(8,128)S(1)} %shard_map.67.update, f32[2,8,64,128]{3,2,1,0:T(8,128)S(1)} %copy-done.1, f32[2,8,64,128]{3,2,1,0:T(8,128)S(1)} %collective-permute-done.2.refs_0_, f32[2,8,64,128]{3,2,1,0:T(8,128)S(1)} %collective-permute-done.3.refs_1_, ...), custom_call_target="tpu_custom_call" | custom-call | tf_op jit(solution)/shard_map/pallas_call | solution.py:503
  (13 shorter events, 0.0 us)
Async XLA Ops:
  0.0 9.2 %copy-start = (f32[2,8,64,128]{3,2,1,0:T(8,128)S(1)}, f32[2,8,64,128]{3,2,1,0:T(8,128)}, u32[]{:S(2)}) copy-start(f32[2,8,64,128]{3,2,1,0:T(8,128)} %own.3) | copy-start | bytes 1572868
  0.0 16.7 %collective-permute-start.2 = (f32[2,8,64,128]{3,2,1,0:T(8,128)}, f32[2,8,64,128]{3,2,1,0:T(8,128)S(1)}, u32[]{:S(2)}, u32[]{:S(2)}) collective-permute-start(f32[2,8,64,128]{3,2,1,0:T(8,128)} %own.3), channel_id=1, source_target_pairs={{0,2},{3,1},{2,3},{1,0},{4,6},{7,5},{6,7},{5,4},{8,10},{11,9},{10,... | collective-permute-start | bytes 1572872 | tf_op jit(solution)/shard_map/ppermute | solution.py:367
  6.5 15.9 %collective-permute-start = (f32[11,64,128]{2,1,0:T(8,128)S(1)}, f32[11,64,128]{2,1,0:T(8,128)}, u32[]{:S(2)}, u32[]{:S(2)}) collective-permute-start(f32[11,64,128]{2,1,0:T(8,128)S(1)} %get-tuple-element.15.up), channel_id=1, source_target_pairs={{0,4},{4,8},{8,12},{12,16},{16,20},{20,24},{24,28},{28,0},{1,5},{5... | collective-permute-start | bytes 1081352 | tf_op jit(solution)/shard_map/ppermute | solution.py:441
  6.5 15.9 %copy-start.3 = (f32[8,64,128]{2,1,0:T(8,128)S(1)}, f32[8,64,128]{2,1,0:T(8,128)}, u32[]{:S(2)}) copy-start(f32[8,64,128]{2,1,0:T(8,128)} %potential.1) | copy-start | bytes 786436
  6.5 15.8 %collective-permute-start.1 = (f32[11,64,128]{2,1,0:T(8,128)}, f32[11,64,128]{2,1,0:T(8,128)}, u32[]{:S(2)}, u32[]{:S(2)}) collective-permute-start(f32[11,64,128]{2,1,0:T(8,128)} %get-tuple-element.16.down), channel_id=1, source_target_pairs={{4,0},{8,4},{12,8},{16,12},{20,16},{24,20},{28,24},{0,28},{5,1},{9... | collective-permute-start | bytes 1081352 | tf_op jit(solution)/shard_map/ppermute | solution.py:442
  9.2 31.0 %collective-permute-start.3 = (f32[2,8,64,128]{3,2,1,0:T(8,128)S(1)}, f32[2,8,64,128]{3,2,1,0:T(8,128)S(1)}, u32[]{:S(2)}, u32[]{:S(2)}) collective-permute-start(f32[2,8,64,128]{3,2,1,0:T(8,128)S(1)} %copy-done), channel_id=1, source_target_pairs={{1,3},{2,0},{0,1},{3,2},{5,7},{6,4},{4,5},{7,6},{9,11},{10,8},{8,9... | collective-permute-start | bytes 1572872 | tf_op jit(solution)/shard_map/ppermute | solution.py:368
  9.2 31.3 %collective-permute-start.4 = (f32[2,8,64,128]{3,2,1,0:T(8,128)S(1)}, f32[2,8,64,128]{3,2,1,0:T(8,128)S(1)}, u32[]{:S(2)}, u32[]{:S(2)}) collective-permute-start(f32[2,8,64,128]{3,2,1,0:T(8,128)S(1)} %copy-done), channel_id=1, source_target_pairs={{1,2},{2,1},{0,0},{3,3},{5,6},{6,5},{4,4},{7,7},{9,10},{10,9},{8,8... | collective-permute-start | bytes 1572872 | tf_op jit(solution)/shard_map/ppermute | solution.py:369
  16.7 23.8 %collective-permute-start.5 = (f32[2,8,64,128]{3,2,1,0:T(8,128)S(1)}, f32[2,8,64,128]{3,2,1,0:T(8,128)S(1)}, u32[]{:S(2)}, u32[]{:S(2)}) collective-permute-start(f32[2,8,64,128]{3,2,1,0:T(8,128)S(1)} %collective-permute-done.2.refs_0_), channel_id=1, source_target_pairs={{2,3},{1,0},{0,1},{3,2},{6,7},{5,4},{4,5},{7,6},{10,11},{9,8},{8,9... | collective-permute-start | bytes 1572872 | tf_op jit(solution)/shard_map/ppermute | solution.py:370
  20.8 0.8 %copy-start.4 = (f32[2,8,64,128]{3,2,1,0:T(8,128)}, f32[2,8,64,128]{3,2,1,0:T(8,128)S(1)}, u32[]{:S(2)}) copy-start(f32[2,8,64,128]{3,2,1,0:T(8,128)S(1)} %get-tuple-element.13.own_scaled) | copy-start | bytes 1572868
  21.6 0.8 %copy-start.5 = (f32[2,8,64,128]{3,2,1,0:T(8,128)}, f32[2,8,64,128]{3,2,1,0:T(8,128)S(1)}, u32[]{:S(2)}) copy-start(f32[2,8,64,128]{3,2,1,0:T(8,128)S(1)} %get-tuple-element.14.own_weight) | copy-start | bytes 1572868
  22.4 0.7 %copy-start.6 = (f32[8]{0:T(128)S(1)}, f32[8]{0:T(128)}, u32[]{:S(2)}) copy-start(f32[8]{0:T(128)} %shifts.3) | copy-start | bytes 100
  22.4 0.7 %copy-start.7 = (s32[2]{0:T(128)S(1)}, s32[2]{0:T(128)}, u32[]{:S(2)}) copy-start(s32[2]{0:T(128)} %assigned.3) | copy-start | bytes 28
  25.8 10.6 %copy-start.2 = (f32[2,8,64,128]{3,2,1,0:T(8,128)S(1)}, f32[2,8,64,128]{3,2,1,0:T(8,128)}, u32[]{:S(2)}) copy-start(f32[2,8,64,128]{3,2,1,0:T(8,128)} %guess.1) | copy-start | bytes 1572868
  36.3 3.9 %copy-start.1 = (f32[2,8,64,128]{3,2,1,0:T(8,128)S(1)}, f32[2,8,64,128]{3,2,1,0:T(8,128)}, u32[]{:S(2)}) copy-start(f32[2,8,64,128]{3,2,1,0:T(8,128)} %own.3) | copy-start | bytes 1572868
  40.7 1.3 %collective-permute-start.6 = (f32[16,128]{1,0:T(8,128)S(1)}, f32[16,128]{1,0:T(8,128)S(1)}, u32[]{:S(2)}, u32[]{:S(2)}) collective-permute-start(f32[16,128]{1,0:T(8,128)S(1)} %shard_map.69), channel_id=1, source_target_pairs={{0,4},{4,0},{8,12},{12,8},{16,20},{20,16},{24,28},{28,24},{1,5},{5... | collective-permute-start | bytes 24584 | tf_op jit(solution)/shard_map/ppermute | solution.py:391
  42.0 4.5 %collective-permute-start.7 = (f32[16,128]{1,0:T(8,128)S(1)}, f32[16,128]{1,0:T(8,128)S(1)}, u32[]{:S(2)}, u32[]{:S(2)}) collective-permute-start(f32[16,128]{1,0:T(8,128)S(1)} %add.3.refs_4_), channel_id=1, source_target_pairs={{0,24},{4,28},{8,16},{12,20},{16,8},{20,12},{24,0},{28,4},{1,25},{... | collective-permute-start | bytes 24584 | tf_op jit(solution)/shard_map/ppermute | solution.py:391
  43.4 3.7 %collective-permute-start.8 = (f32[16,128]{1,0:T(8,128)S(1)}, f32[16,128]{1,0:T(8,128)S(1)}, u32[]{:S(2)}, u32[]{:S(2)}) collective-permute-start(f32[16,128]{1,0:T(8,128)S(1)} %add.3.refs_4_), channel_id=1, source_target_pairs={{0,16},{4,20},{8,24},{12,28},{16,0},{20,4},{24,8},{28,12},{1,17},{... | collective-permute-start | bytes 24584 | tf_op jit(solution)/shard_map/ppermute | solution.py:391
  44.9 3.7 %collective-permute-start.9 = (f32[16,128]{1,0:T(8,128)S(1)}, f32[16,128]{1,0:T(8,128)S(1)}, u32[]{:S(2)}, u32[]{:S(2)}) collective-permute-start(f32[16,128]{1,0:T(8,128)S(1)} %add.3.refs_4_), channel_id=1, source_target_pairs={{0,8},{4,12},{8,0},{12,4},{16,24},{20,28},{24,16},{28,20},{1,9},{5... | collective-permute-start | bytes 24584 | tf_op jit(solution)/shard_map/ppermute | solution.py:391

commit v3 on v2

--- a/solution.py
+++ b/solution.py
@@ -326,11 +326,18 @@
     row_sums([reader(ref) for ref in (own,) + refs[:-1]], update, refs[-1], 0)
 
 
+def lane_of(rows):
+    place = (rows, LANES)
+    return lax.broadcasted_iota(jnp.int32, place, 0) == lax.broadcasted_iota(jnp.int32, place, 1)
+
+
 def late_kernel(outside, update, early, *refs):
-    last, out = refs[:-1], refs[-1]
+    last, (out, sums) = refs[:-2], refs[-2:]
     rows = early.shape[0]
-    out[0:rows] = early[...]
-    row_sums([reader(*last, *chosen(last, outside))], update, out, rows)
+    sums[0:rows] = early[...]
+    row_sums([reader(*last, *chosen(last, outside))], update, sums, rows)
+    total = jnp.sum(sums[...], axis=1, keepdims=True)
+    out[...] = jnp.sum(jnp.where(lane_of(sums.shape[0]), total, 0.0), axis=0, keepdims=True)
 
 
 def project_kernel(blocks, parts, cells, outside, update, own, *refs):
@@ -340,7 +347,9 @@
     total = sums[0][...]
     for part in sums[1:]:
         total = total + part[...]
-    overlap = jnp.sum(total, axis=1, keepdims=True) / cells
+    pairs = (2 + blocks) * count * count
+    spread = jnp.where(lane_of(pairs), jnp.broadcast_to(total, (pairs, LANES)), 0.0)
+    overlap = jnp.sum(spread, axis=1, keepdims=True) / cells
     reads = [reader(ref) for ref in (own,) + others] + [reader(*last, *chosen(last, outside))]
 
     def store(x):
@@ -379,17 +388,17 @@
     n = lax.axis_size(axis)
     if n & (n - 1):
         return [lax.psum(value, axis)]
-    parts, stride, width = [value], 1, 2
-    while stride < n:
+    parts, top = [value], n
+    while top > 1:
         total = parts[0]
         for part in parts[1:]:
             total = total + part
-        width = min(width, n // stride)
+        width = min(4, top // 2) if top > 2 else 2
+        top //= width
         parts = [total]
         for k in range(width - 1, 0, -1):
-            pairs = [(i, i ^ (k * stride)) for i in range(n)]
+            pairs = [(i, i ^ (k * top)) for i in range(n)]
             parts.append(lax.ppermute(total, axis, pairs))
-        stride, width = stride * width, 4
     return parts
 
 
@@ -493,9 +502,10 @@
     )(update, orbitals, *blocks)
     sums = pl.pallas_call(
         late_kernel,
-        out_shape=shape(rows + count * count, LANES),
+        out_shape=shape(1, LANES),
         in_specs=[SMEM] + [VMEM] * (2 + len(last)),
         out_specs=VMEM,
+        scratch_shapes=[scratch(rows + count * count, LANES)],
         compiler_params=params,
     )(outside, update, sums, *last)
     parts = reduce_parts(sums, "dom")

time: 49.9 us -> 49.8 us (level)
  no operation moved by 1% of the time
where the time goes in v3:
time: 49.8 us; the launch traced here: 49.6 us
  starting transfers between devices  13.2 us (27%)
  Pallas kernels  12.4 us (25%)
  waiting for transfers between devices  11.1 us (22%)
  blocking collectives  10.5 us (21%)
  local copies, waits for them, and re-layouts  2.25 us (5%)
    all_gather x1, blocking collectives, on_device(): gathered = lax.all_gather(payload, 'dom', axis=0)  10.5 us
    ppermute x1, waiting for transfers between devices, gather_blocks(): first = lax.ppermute(block, axis, [(0, 2), (3, 1), (2, 3), (1, 0)])  6.88 us
    ppermute x4, waiting for transfers between devices, reduce_parts(): parts.append(lax.ppermute(total, axis, pairs))  4.19 us
    ppermute x1, starting transfers between devices, gather_blocks(): first = lax.ppermute(block, axis, [(0, 2), (3, 1), (2, 3), (1, 0)])  4.06 us
    pallas_call x1, Pallas kernels, on_device(): pl.pallas_call(coarse_kernel, out_shape=shape(count, depth, *plane), in_s...  3.85 us
    ppermute x4, starting transfers between devices, reduce_parts(): parts.append(lax.ppermute(total, axis, pairs))  3.49 us
    pallas_call x1, Pallas kernels, on_device(): pl.pallas_call(fine_kernel, out_shape=(shape(count, depth + 4, *plane), s...  2.7 us
    ppermute x1, starting transfers between devices, on_device(): lax.ppermute(down, 'dom', [((i + 1) % members, i) for i in range(members)])  2.62 us
  transfers between devices with their start and end apart: 10, of which 5 were waited for; matrix products, arithmetic and copies ran while one was open for 0% of the time, Pallas kernels for 22%

profile of v3, /device:TPU:0, one launch (start us, length us, event | category | flops | bytes accessed | tf_op | source)
XLA Modules:
  0.0 49.6 jit_solution(7029784520972180120)
XLA Ops:
  0.0 4.1 %collective-permute-start.2 = (f32[2,8,64,128]{3,2,1,0:T(8,128)}, f32[2,8,64,128]{3,2,1,0:T(8,128)S(1)}, u32[]{:S(2)}, u32[]{:S(2)}) collective-permute-start(f32[2,8,64,128]{3,2,1,0:T(8,128)} %own.3), channel_id=1, source_target_pairs={{0,2},{3,1},{2,3},{1,0},{4,6},{7,5},{6,7},{5,4},{8,10},{11,9},{10,... | collective-permute-start | bytes 1572872 | tf_op jit(solution)/shard_map/ppermute | solution.py:376
  4.1 2.4 %shard_map.65 = (f32[11,64,128]{2,1,0:T(8,128)S(1)}, f32[11,64,128]{2,1,0:T(8,128)}) custom-call(f32[8]{0:T(128)} %shifts.3, s32[2]{0:T(128)} %assigned.3, f32[2,8,64,128]{3,2,1,0:T(8,128)} %guess.1, f32[2,8,64,128]{3,2,1,0:T(8,128)} %own.3, f32[8,64,128]{2,1,0:T(8,128)} %potential.1, f32[8,64,128]{2,1,0:T(8,128)} %perturbation_in.3), custom_call_target="tpu_custom_call" | custom-call | tf_op jit(solution)/shard_map/pallas_call | solution.py:434
  6.5 0.1 collective-permute-start
  6.5 0.0 copy-start.3
  6.5 2.6 %collective-permute-start.1 = (f32[11,64,128]{2,1,0:T(8,128)}, f32[11,64,128]{2,1,0:T(8,128)}, u32[]{:S(2)}, u32[]{:S(2)}) collective-permute-start(f32[11,64,128]{2,1,0:T(8,128)} %get-tuple-element.16.down), channel_id=1, source_target_pairs={{4,0},{8,4},{12,8},{16,12},{20,16},{24,20},{28,24},{0,28},{5,1},{9... | collective-permute-start | bytes 1081352 | tf_op jit(solution)/shard_map/ppermute | solution.py:451
  9.2 0.0 collective-permute-start.3
  9.2 0.7 %collective-permute-start.4 = (f32[2,8,64,128]{3,2,1,0:T(8,128)S(1)}, f32[2,8,64,128]{3,2,1,0:T(8,128)S(1)}, u32[]{:S(2)}, u32[]{:S(2)}) collective-permute-start(f32[2,8,64,128]{3,2,1,0:T(8,128)S(1)} %copy-done), channel_id=1, source_target_pairs={{1,2},{2,1},{0,0},{3,3},{5,6},{6,5},{4,4},{7,7},{9,10},{10,9},{8,8... | collective-permute-start | bytes 1572872 | tf_op jit(solution)/shard_map/ppermute | solution.py:378
  9.9 6.9 %collective-permute-done.2.refs_0_ = f32[2,8,64,128]{3,2,1,0:T(8,128)S(1)} collective-permute-done((f32[2,8,64,128]{3,2,1,0:T(8,128)}, f32[2,8,64,128]{3,2,1,0:T(8,128)S(1)}, u32[]{:S(2)}, u32[]{:S(2)}) %collective-permute-start.2) | collective-permute-done | bytes 524320 | tf_op jit(solution)/shard_map/ppermute | solution.py:376
  16.7 2.3 %collective-permute-start.5 = (f32[2,8,64,128]{3,2,1,0:T(8,128)S(1)}, f32[2,8,64,128]{3,2,1,0:T(8,128)S(1)}, u32[]{:S(2)}, u32[]{:S(2)}) collective-permute-start(f32[2,8,64,128]{3,2,1,0:T(8,128)S(1)} %collective-permute-done.2.refs_0_), channel_id=1, source_target_pairs={{2,3},{1,0},{0,1},{3,2},{6,7},{5,4},{4,5},{7,6},{10,11},{9,8},{8,9... | collective-permute-start | bytes 1572872 | tf_op jit(solution)/shard_map/ppermute | solution.py:379
  19.0 1.8 %shard_map.64 = (f32[2,8,64,128]{3,2,1,0:T(8,128)S(1)}, f32[2,8,64,128]{3,2,1,0:T(8,128)S(1)}) custom-call(f32[8]{0:T(128)} %shifts.3, s32[2]{0:T(128)} %assigned.3, f32[2,8,64,128]{3,2,1,0:T(8,128)} %guess.1, f32[2,8,64,128]{3,2,1,0:T(8,128)} %own.3, f32[8,64,128]{2,1,0:T(8,128)} %potential.1, f32[8,64,128]{2,1,0:T(8,128)} %perturbation_in.3), custom_call_target="tpu_custom_call" | custom-call | tf_op jit(solution)/shard_map/pallas_call | solution.py:442
  20.8 0.0 copy-start.4
  20.8 0.8 %copy-done.4 = f32[2,8,64,128]{3,2,1,0:T(8,128)} copy-done((f32[2,8,64,128]{3,2,1,0:T(8,128)}, f32[2,8,64,128]{3,2,1,0:T(8,128)S(1)}, u32[]{:S(2)}) %copy-start.4) | copy-done | bytes 524312
  21.6 0.8 %copy-done.5 = f32[2,8,64,128]{3,2,1,0:T(8,128)} copy-done((f32[2,8,64,128]{3,2,1,0:T(8,128)}, f32[2,8,64,128]{3,2,1,0:T(8,128)S(1)}, u32[]{:S(2)}) %copy-start.5) | copy-done | bytes 524312
  22.4 0.0 collective-permute-done.low
  22.4 0.0 copy-start.7
  22.4 0.6 %copy-done.6 = f32[8]{0:T(128)S(1)} copy-done((f32[8]{0:T(128)S(1)}, f32[8]{0:T(128)}, u32[]{:S(2)}) %copy-start.6) | copy-done | bytes 56
  23.0 0.0 copy-done.7
  23.1 2.7 %shard_map.66 = (f32[2,12,64,128]{3,2,1,0:T(8,128)S(1)}, f32[2,10,64,128]{3,2,1,0:T(8,128)S(1)}, f32[2,10,64,128]{3,2,1,0:T(8,128)S(1)}, f32[6,32,128]{2,1,0:T(8,128)S(1)}) custom-call(f32[8]{0:T(128)S(1)} %copy-done.6, s32[2]{0:T(128)S(1)} %copy-done.7, f32[2,8,64,128]{3,2,1,0:T(8,128)} %copy-done.4, f32[2,8,64,128]{3,2,1,0:T(8,128)} %copy-done.5, ...), custom_call_target="tpu_custom_call" | custom-call | tf_op jit(solution)/shard_map/pallas_call | solution.py:453
  25.8 0.0 copy-start.2
  25.8 10.5 %all-gather = f32[48,32,128]{2,1,0:T(8,128)S(1)} all-gather(f32[6,32,128]{2,1,0:T(8,128)S(1)} %get-tuple-element.17), channel_id=2, replica_groups=mesh['dom'=8,'orb'=4] {'dom'}, dimensions={0}, use_global_device_ids=true | all-gather | bytes 884736 | tf_op jit(solution)/shard_map/all_gather | solution.py:471
  36.3 3.8 %shard_map.67.update = f32[2,8,64,128]{3,2,1,0:T(8,128)S(1)} custom-call(s32[1]{0:T(128)} %bitcast.1.place, f32[8]{0:T(128)S(1)} %copy-done.6, s32[2]{0:T(128)S(1)} %copy-done.7, f32[8,6,32,128]{3,2,1,0:T(8,128)S(1)} %bitcast.3, f32[2,12,64,128]{3,2,1,0:T(8,128)S(1)} %get-tuple-element.18.estimate, f32[2,10,64,128]{3,2,1,0:T(8,128)S(1)} %get-tuple-element.19.scaled, ...), custom_call_target="tpu_custom_call" | custom-call | tf_op jit(solution)/shard_map/pallas_call | solution.py:474
  40.2 0.3 shard_map.68.early
  40.5 0.0 collective-permute-done.4.refs_0_.refs_2_
  40.5 0.3 shard_map.69
  40.8 1.5 %collective-permute-start.6 = (f32[1,128]{1,0:T(1,128)S(1)}, f32[1,128]{1,0:T(1,128)S(1)}, u32[]{:S(2)}, u32[]{:S(2)}) collective-permute-start(f32[1,128]{1,0:T(1,128)S(1)} %shard_map.69), channel_id=1, source_target_pairs={{0,24},{4,28},{8,16},{12,20},{16,8},{20,12},{24,0},{28,4},{1,25},{... | collective-permute-start | bytes 1544 | tf_op jit(solution)/shard_map/ppermute | solution.py:401
  42.3 1.5 %collective-permute-start.7 = (f32[1,128]{1,0:T(1,128)S(1)}, f32[1,128]{1,0:T(1,128)S(1)}, u32[]{:S(2)}, u32[]{:S(2)}) collective-permute-start(f32[1,128]{1,0:T(1,128)S(1)} %shard_map.69), channel_id=1, source_target_pairs={{0,16},{4,20},{8,24},{12,28},{16,0},{20,4},{24,8},{28,12},{1,17},{... | collective-permute-start | bytes 1544 | tf_op jit(solution)/shard_map/ppermute | solution.py:401
  43.7 0.5 %collective-permute-start.8 = (f32[1,128]{1,0:T(1,128)S(1)}, f32[1,128]{1,0:T(1,128)S(1)}, u32[]{:S(2)}, u32[]{:S(2)}) collective-permute-start(f32[1,128]{1,0:T(1,128)S(1)} %shard_map.69), channel_id=1, source_target_pairs={{0,8},{4,12},{8,0},{12,4},{16,24},{20,28},{24,16},{28,20},{1,9},{5... | collective-permute-start | bytes 1544 | tf_op jit(solution)/shard_map/ppermute | solution.py:401
  44.3 1.0 %collective-permute-done.6 = f32[1,128]{1,0:T(1,128)S(1)} collective-permute-done((f32[1,128]{1,0:T(1,128)S(1)}, f32[1,128]{1,0:T(1,128)S(1)}, u32[]{:S(2)}, u32[]{:S(2)}) %collective-permute-start.6) | collective-permute-done | bytes 544 | tf_op jit(solution)/shard_map/ppermute | solution.py:401
  45.3 0.6 %collective-permute-done.7 = f32[1,128]{1,0:T(1,128)S(1)} collective-permute-done((f32[1,128]{1,0:T(1,128)S(1)}, f32[1,128]{1,0:T(1,128)S(1)}, u32[]{:S(2)}, u32[]{:S(2)}) %collective-permute-start.7) | collective-permute-done | bytes 544 | tf_op jit(solution)/shard_map/ppermute | solution.py:401
  45.8 1.5 %collective-permute-done.8 = f32[1,128]{1,0:T(1,128)S(1)} collective-permute-done((f32[1,128]{1,0:T(1,128)S(1)}, f32[1,128]{1,0:T(1,128)S(1)}, u32[]{:S(2)}, u32[]{:S(2)}) %collective-permute-start.8) | collective-permute-done | bytes 544 | tf_op jit(solution)/shard_map/ppermute | solution.py:401
  47.3 1.2 %collective-permute-done.9.refs_5_ = f32[1,128]{1,0:T(1,128)S(1)} collective-permute-done((f32[1,128]{1,0:T(1,128)S(1)}, f32[1,128]{1,0:T(1,128)S(1)}, u32[]{:S(2)}, u32[]{:S(2)}) %collective-permute-start.9) | collective-permute-done | bytes 544 | tf_op jit(solution)/shard_map/ppermute | solution.py:401
  48.5 1.1 %shard_map.70 = f32[2,8,64,128]{3,2,1,0:T(8,128)} custom-call(s32[1]{0:T(128)} %bitcast.outside, f32[2,8,64,128]{3,2,1,0:T(8,128)S(1)} %shard_map.67.update, f32[2,8,64,128]{3,2,1,0:T(8,128)S(1)} %copy-done.1, f32[2,8,64,128]{3,2,1,0:T(8,128)S(1)} %collective-permute-done.2.refs_0_, f32[2,8,64,128]{3,2,1,0:T(8,128)S(1)} %collective-permute-done.3.refs_1_, ...), custom_call_target="tpu_custom_call" | custom-call | tf_op jit(solution)/shard_map/pallas_call | solution.py:513
  (13 shorter events, 0.0 us)
Async XLA Ops:
  0.0 9.2 %copy-start = (f32[2,8,64,128]{3,2,1,0:T(8,128)S(1)}, f32[2,8,64,128]{3,2,1,0:T(8,128)}, u32[]{:S(2)}) copy-start(f32[2,8,64,128]{3,2,1,0:T(8,128)} %own.3) | copy-start | bytes 1572868
  0.0 16.7 %collective-permute-start.2 = (f32[2,8,64,128]{3,2,1,0:T(8,128)}, f32[2,8,64,128]{3,2,1,0:T(8,128)S(1)}, u32[]{:S(2)}, u32[]{:S(2)}) collective-permute-start(f32[2,8,64,128]{3,2,1,0:T(8,128)} %own.3), channel_id=1, source_target_pairs={{0,2},{3,1},{2,3},{1,0},{4,6},{7,5},{6,7},{5,4},{8,10},{11,9},{10,... | collective-permute-start | bytes 1572872 | tf_op jit(solution)/shard_map/ppermute | solution.py:376
  6.5 15.9 %collective-permute-start = (f32[11,64,128]{2,1,0:T(8,128)S(1)}, f32[11,64,128]{2,1,0:T(8,128)}, u32[]{:S(2)}, u32[]{:S(2)}) collective-permute-start(f32[11,64,128]{2,1,0:T(8,128)S(1)} %get-tuple-element.15.up), channel_id=1, source_target_pairs={{0,4},{4,8},{8,12},{12,16},{16,20},{20,24},{24,28},{28,0},{1,5},{5... | collective-permute-start | bytes 1081352 | tf_op jit(solution)/shard_map/ppermute | solution.py:450
  6.5 15.9 %copy-start.3 = (f32[8,64,128]{2,1,0:T(8,128)S(1)}, f32[8,64,128]{2,1,0:T(8,128)}, u32[]{:S(2)}) copy-start(f32[8,64,128]{2,1,0:T(8,128)} %potential.1) | copy-start | bytes 786436
  6.5 15.8 %collective-permute-start.1 = (f32[11,64,128]{2,1,0:T(8,128)}, f32[11,64,128]{2,1,0:T(8,128)}, u32[]{:S(2)}, u32[]{:S(2)}) collective-permute-start(f32[11,64,128]{2,1,0:T(8,128)} %get-tuple-element.16.down), channel_id=1, source_target_pairs={{4,0},{8,4},{12,8},{16,12},{20,16},{24,20},{28,24},{0,28},{5,1},{9... | collective-permute-start | bytes 1081352 | tf_op jit(solution)/shard_map/ppermute | solution.py:451
  9.2 31.0 %collective-permute-start.3 = (f32[2,8,64,128]{3,2,1,0:T(8,128)S(1)}, f32[2,8,64,128]{3,2,1,0:T(8,128)S(1)}, u32[]{:S(2)}, u32[]{:S(2)}) collective-permute-start(f32[2,8,64,128]{3,2,1,0:T(8,128)S(1)} %copy-done), channel_id=1, source_target_pairs={{1,3},{2,0},{0,1},{3,2},{5,7},{6,4},{4,5},{7,6},{9,11},{10,8},{8,9... | collective-permute-start | bytes 1572872 | tf_op jit(solution)/shard_map/ppermute | solution.py:377
  9.2 31.3 %collective-permute-start.4 = (f32[2,8,64,128]{3,2,1,0:T(8,128)S(1)}, f32[2,8,64,128]{3,2,1,0:T(8,128)S(1)}, u32[]{:S(2)}, u32[]{:S(2)}) collective-permute-start(f32[2,8,64,128]{3,2,1,0:T(8,128)S(1)} %copy-done), channel_id=1, source_target_pairs={{1,2},{2,1},{0,0},{3,3},{5,6},{6,5},{4,4},{7,7},{9,10},{10,9},{8,8... | collective-permute-start | bytes 1572872 | tf_op jit(solution)/shard_map/ppermute | solution.py:378
  16.7 23.8 %collective-permute-start.5 = (f32[2,8,64,128]{3,2,1,0:T(8,128)S(1)}, f32[2,8,64,128]{3,2,1,0:T(8,128)S(1)}, u32[]{:S(2)}, u32[]{:S(2)}) collective-permute-start(f32[2,8,64,128]{3,2,1,0:T(8,128)S(1)} %collective-permute-done.2.refs_0_), channel_id=1, source_target_pairs={{2,3},{1,0},{0,1},{3,2},{6,7},{5,4},{4,5},{7,6},{10,11},{9,8},{8,9... | collective-permute-start | bytes 1572872 | tf_op jit(solution)/shard_map/ppermute | solution.py:379
  20.8 0.8 %copy-start.4 = (f32[2,8,64,128]{3,2,1,0:T(8,128)}, f32[2,8,64,128]{3,2,1,0:T(8,128)S(1)}, u32[]{:S(2)}) copy-start(f32[2,8,64,128]{3,2,1,0:T(8,128)S(1)} %get-tuple-element.13.own_scaled) | copy-start | bytes 1572868
  21.6 0.8 %copy-start.5 = (f32[2,8,64,128]{3,2,1,0:T(8,128)}, f32[2,8,64,128]{3,2,1,0:T(8,128)S(1)}, u32[]{:S(2)}) copy-start(f32[2,8,64,128]{3,2,1,0:T(8,128)S(1)} %get-tuple-element.14.own_weight) | copy-start | bytes 1572868
  22.4 0.7 %copy-start.6 = (f32[8]{0:T(128)S(1)}, f32[8]{0:T(128)}, u32[]{:S(2)}) copy-start(f32[8]{0:T(128)} %shifts.3) | copy-start | bytes 100
  22.4 0.7 %copy-start.7 = (s32[2]{0:T(128)S(1)}, s32[2]{0:T(128)}, u32[]{:S(2)}) copy-start(s32[2]{0:T(128)} %assigned.3) | copy-start | bytes 28
  25.8 10.6 %copy-start.2 = (f32[2,8,64,128]{3,2,1,0:T(8,128)S(1)}, f32[2,8,64,128]{3,2,1,0:T(8,128)}, u32[]{:S(2)}) copy-start(f32[2,8,64,128]{3,2,1,0:T(8,128)} %guess.1) | copy-start | bytes 1572868
  36.3 3.9 %copy-start.1 = (f32[2,8,64,128]{3,2,1,0:T(8,128)S(1)}, f32[2,8,64,128]{3,2,1,0:T(8,128)}, u32[]{:S(2)}) copy-start(f32[2,8,64,128]{3,2,1,0:T(8,128)} %own.3) | copy-start | bytes 1572868
  40.8 4.5 %collective-permute-start.6 = (f32[1,128]{1,0:T(1,128)S(1)}, f32[1,128]{1,0:T(1,128)S(1)}, u32[]{:S(2)}, u32[]{:S(2)}) collective-permute-start(f32[1,128]{1,0:T(1,128)S(1)} %shard_map.69), channel_id=1, source_target_pairs={{0,24},{4,28},{8,16},{12,20},{16,8},{20,12},{24,0},{28,4},{1,25},{... | collective-permute-start | bytes 1544 | tf_op jit(solution)/shard_map/ppermute | solution.py:401
  42.3 3.6 %collective-permute-start.7 = (f32[1,128]{1,0:T(1,128)S(1)}, f32[1,128]{1,0:T(1,128)S(1)}, u32[]{:S(2)}, u32[]{:S(2)}) collective-permute-start(f32[1,128]{1,0:T(1,128)S(1)} %shard_map.69), channel_id=1, source_target_pairs={{0,16},{4,20},{8,24},{12,28},{16,0},{20,4},{24,8},{28,12},{1,17},{... | collective-permute-start | bytes 1544 | tf_op jit(solution)/shard_map/ppermute | solution.py:401
  43.7 3.6 %collective-permute-start.8 = (f32[1,128]{1,0:T(1,128)S(1)}, f32[1,128]{1,0:T(1,128)S(1)}, u32[]{:S(2)}, u32[]{:S(2)}) collective-permute-start(f32[1,128]{1,0:T(1,128)S(1)} %shard_map.69), channel_id=1, source_target_pairs={{0,8},{4,12},{8,0},{12,4},{16,24},{20,28},{24,16},{28,20},{1,9},{5... | collective-permute-start | bytes 1544 | tf_op jit(solution)/shard_map/ppermute | solution.py:401
  47.3 1.2 %collective-permute-start.9 = (f32[1,128]{1,0:T(1,128)S(1)}, f32[1,128]{1,0:T(1,128)S(1)}, u32[]{:S(2)}, u32[]{:S(2)}) collective-permute-start(f32[1,128]{1,0:T(1,128)S(1)} %add_add_fusion.refs_4_), channel_id=1, source_target_pairs={{0,4},{4,0},{8,12},{12,8},{16,20},{20,16},{24,28},{28,24},{1,5},{5... | collective-permute-start | bytes 1544 | tf_op jit(solution)/shard_map/ppermute | solution.py:401

commit v4 on v3

--- a/solution.py
+++ b/solution.py
@@ -352,8 +352,8 @@
     overlap = jnp.sum(spread, axis=1, keepdims=True) / cells
     reads = [reader(ref) for ref in (own,) + others] + [reader(*last, *chosen(last, outside))]
 
-    def store(x):
-        return pltpu.make_async_copy(out.at[:, x], out_ref.at[:, x], sems.at[x])
+    def store(i, x):
+        return pltpu.make_async_copy(out.at[i, x], out_ref.at[i, x], sems.at[i, x])
 
     for x in range(depth):
         values = [update[i, x] for i in range(count)]
@@ -365,9 +365,10 @@
                     values[i] = values[i] - overlap[k : k + 1] * o
         for i in range(count):
             out[i, x] = values[i]
-        store(x).start()
+            store(i, x).start()
     for x in range(depth):
-        store(x).wait()
+        for i in range(count):
+            store(i, x).wait()
 
 
 def gather_blocks(block, axis):
@@ -515,7 +516,7 @@
         out_shape=shape(count, depth, *plane),
         in_specs=[SMEM] + [VMEM] * (2 + len(blocks) + len(last) + len(parts)),
         out_specs=HBM,
-        scratch_shapes=[scratch(count, depth, *plane), pltpu.SemaphoreType.DMA((depth,))],
+        scratch_shapes=[scratch(count, depth, *plane), pltpu.SemaphoreType.DMA((count, depth))],
         compiler_params=params,
     )(outside, update, orbitals, *blocks, *last, *parts)
 

time: 49.8 us -> 49.9 us (level)
  no operation moved by 1% of the time
where the time goes in v4:
time: 49.9 us; the launch traced here: 49.6 us
  starting transfers between devices  13.2 us (26%)
  Pallas kernels  12.4 us (25%)
  waiting for transfers between devices  11.1 us (22%)
  blocking collectives  10.5 us (21%)
  local copies, waits for them, and re-layouts  2.25 us (5%)
    all_gather x1, blocking collectives, on_device(): gathered = lax.all_gather(payload, 'dom', axis=0)  10.5 us
    ppermute x1, waiting for transfers between devices, gather_blocks(): first = lax.ppermute(block, axis, [(0, 2), (3, 1), (2, 3), (1, 0)])  6.88 us
    ppermute x4, waiting for transfers between devices, reduce_parts(): parts.append(lax.ppermute(total, axis, pairs))  4.19 us
    ppermute x1, starting transfers between devices, gather_blocks(): first = lax.ppermute(block, axis, [(0, 2), (3, 1), (2, 3), (1, 0)])  4.06 us
    pallas_call x1, Pallas kernels, on_device(): pl.pallas_call(coarse_kernel, out_shape=shape(count, depth, *plane), in_s...  3.85 us
    ppermute x4, starting transfers between devices, reduce_parts(): parts.append(lax.ppermute(total, axis, pairs))  3.49 us
    pallas_call x1, Pallas kernels, on_device(): pl.pallas_call(fine_kernel, out_shape=(shape(count, depth + 4, *plane), s...  2.7 us
    ppermute x1, starting transfers between devices, on_device(): lax.ppermute(down, 'dom', [((i + 1) % members, i) for i in range(members)])  2.62 us
  transfers between devices with their start and end apart: 10, of which 5 were waited for; matrix products, arithmetic and copies ran while one was open for 0% of the time, Pallas kernels for 22%

profile of v4, /device:TPU:0, one launch (start us, length us, event | category | flops | bytes accessed | tf_op | source)
XLA Modules:
  0.0 49.6 jit_solution(15158829501659551257)
XLA Ops:
  0.0 4.1 %collective-permute-start.2 = (f32[2,8,64,128]{3,2,1,0:T(8,128)}, f32[2,8,64,128]{3,2,1,0:T(8,128)S(1)}, u32[]{:S(2)}, u32[]{:S(2)}) collective-permute-start(f32[2,8,64,128]{3,2,1,0:T(8,128)} %own.3), channel_id=1, source_target_pairs={{0,2},{3,1},{2,3},{1,0},{4,6},{7,5},{6,7},{5,4},{8,10},{11,9},{10,... | collective-permute-start | bytes 1572872 | tf_op jit(solution)/shard_map/ppermute | solution.py:377
  4.1 2.4 %shard_map.65 = (f32[11,64,128]{2,1,0:T(8,128)S(1)}, f32[11,64,128]{2,1,0:T(8,128)}) custom-call(f32[8]{0:T(128)} %shifts.3, s32[2]{0:T(128)} %assigned.3, f32[2,8,64,128]{3,2,1,0:T(8,128)} %guess.1, f32[2,8,64,128]{3,2,1,0:T(8,128)} %own.3, f32[8,64,128]{2,1,0:T(8,128)} %potential.1, f32[8,64,128]{2,1,0:T(8,128)} %perturbation_in.3), custom_call_target="tpu_custom_call" | custom-call | tf_op jit(solution)/shard_map/pallas_call | solution.py:435
  6.5 0.1 collective-permute-start
  6.5 0.0 copy-start.3
  6.5 2.6 %collective-permute-start.1 = (f32[11,64,128]{2,1,0:T(8,128)}, f32[11,64,128]{2,1,0:T(8,128)}, u32[]{:S(2)}, u32[]{:S(2)}) collective-permute-start(f32[11,64,128]{2,1,0:T(8,128)} %get-tuple-element.16.down), channel_id=1, source_target_pairs={{4,0},{8,4},{12,8},{16,12},{20,16},{24,20},{28,24},{0,28},{5,1},{9... | collective-permute-start | bytes 1081352 | tf_op jit(solution)/shard_map/ppermute | solution.py:452
  9.2 0.0 collective-permute-start.3
  9.2 0.7 %collective-permute-start.4 = (f32[2,8,64,128]{3,2,1,0:T(8,128)S(1)}, f32[2,8,64,128]{3,2,1,0:T(8,128)S(1)}, u32[]{:S(2)}, u32[]{:S(2)}) collective-permute-start(f32[2,8,64,128]{3,2,1,0:T(8,128)S(1)} %copy-done), channel_id=1, source_target_pairs={{1,2},{2,1},{0,0},{3,3},{5,6},{6,5},{4,4},{7,7},{9,10},{10,9},{8,8... | collective-permute-start | bytes 1572872 | tf_op jit(solution)/shard_map/ppermute | solution.py:379
  9.9 6.9 %collective-permute-done.2.refs_0_ = f32[2,8,64,128]{3,2,1,0:T(8,128)S(1)} collective-permute-done((f32[2,8,64,128]{3,2,1,0:T(8,128)}, f32[2,8,64,128]{3,2,1,0:T(8,128)S(1)}, u32[]{:S(2)}, u32[]{:S(2)}) %collective-permute-start.2) | collective-permute-done | bytes 524320 | tf_op jit(solution)/shard_map/ppermute | solution.py:377
  16.7 2.3 %collective-permute-start.5 = (f32[2,8,64,128]{3,2,1,0:T(8,128)S(1)}, f32[2,8,64,128]{3,2,1,0:T(8,128)S(1)}, u32[]{:S(2)}, u32[]{:S(2)}) collective-permute-start(f32[2,8,64,128]{3,2,1,0:T(8,128)S(1)} %collective-permute-done.2.refs_0_), channel_id=1, source_target_pairs={{2,3},{1,0},{0,1},{3,2},{6,7},{5,4},{4,5},{7,6},{10,11},{9,8},{8,9... | collective-permute-start | bytes 1572872 | tf_op jit(solution)/shard_map/ppermute | solution.py:380
  19.0 1.8 %shard_map.64 = (f32[2,8,64,128]{3,2,1,0:T(8,128)S(1)}, f32[2,8,64,128]{3,2,1,0:T(8,128)S(1)}) custom-call(f32[8]{0:T(128)} %shifts.3, s32[2]{0:T(128)} %assigned.3, f32[2,8,64,128]{3,2,1,0:T(8,128)} %guess.1, f32[2,8,64,128]{3,2,1,0:T(8,128)} %own.3, f32[8,64,128]{2,1,0:T(8,128)} %potential.1, f32[8,64,128]{2,1,0:T(8,128)} %perturbation_in.3), custom_call_target="tpu_custom_call" | custom-call | tf_op jit(solution)/shard_map/pallas_call | solution.py:443
  20.8 0.0 copy-start.4
  20.8 0.8 %copy-done.4 = f32[2,8,64,128]{3,2,1,0:T(8,128)} copy-done((f32[2,8,64,128]{3,2,1,0:T(8,128)}, f32[2,8,64,128]{3,2,1,0:T(8,128)S(1)}, u32[]{:S(2)}) %copy-start.4) | copy-done | bytes 524312
  21.6 0.8 %copy-done.5 = f32[2,8,64,128]{3,2,1,0:T(8,128)} copy-done((f32[2,8,64,128]{3,2,1,0:T(8,128)}, f32[2,8,64,128]{3,2,1,0:T(8,128)S(1)}, u32[]{:S(2)}) %copy-start.5) | copy-done | bytes 524312
  22.4 0.0 collective-permute-done.low
  22.4 0.0 copy-start.7
  22.4 0.6 %copy-done.6 = f32[8]{0:T(128)S(1)} copy-done((f32[8]{0:T(128)S(1)}, f32[8]{0:T(128)}, u32[]{:S(2)}) %copy-start.6) | copy-done | bytes 56
  23.0 0.0 copy-done.7
  23.1 2.7 %shard_map.66 = (f32[2,12,64,128]{3,2,1,0:T(8,128)S(1)}, f32[2,10,64,128]{3,2,1,0:T(8,128)S(1)}, f32[2,10,64,128]{3,2,1,0:T(8,128)S(1)}, f32[6,32,128]{2,1,0:T(8,128)S(1)}) custom-call(f32[8]{0:T(128)S(1)} %copy-done.6, s32[2]{0:T(128)S(1)} %copy-done.7, f32[2,8,64,128]{3,2,1,0:T(8,128)} %copy-done.4, f32[2,8,64,128]{3,2,1,0:T(8,128)} %copy-done.5, ...), custom_call_target="tpu_custom_call" | custom-call | tf_op jit(solution)/shard_map/pallas_call | solution.py:454
  25.8 0.0 copy-start.2
  25.8 10.5 %all-gather = f32[48,32,128]{2,1,0:T(8,128)S(1)} all-gather(f32[6,32,128]{2,1,0:T(8,128)S(1)} %get-tuple-element.17), channel_id=2, replica_groups=mesh['dom'=8,'orb'=4] {'dom'}, dimensions={0}, use_global_device_ids=true | all-gather | bytes 884736 | tf_op jit(solution)/shard_map/all_gather | solution.py:472
  36.3 3.8 %shard_map.67.update = f32[2,8,64,128]{3,2,1,0:T(8,128)S(1)} custom-call(s32[1]{0:T(128)} %bitcast.1.place, f32[8]{0:T(128)S(1)} %copy-done.6, s32[2]{0:T(128)S(1)} %copy-done.7, f32[8,6,32,128]{3,2,1,0:T(8,128)S(1)} %bitcast.3, f32[2,12,64,128]{3,2,1,0:T(8,128)S(1)} %get-tuple-element.18.estimate, f32[2,10,64,128]{3,2,1,0:T(8,128)S(1)} %get-tuple-element.19.scaled, ...), custom_call_target="tpu_custom_call" | custom-call | tf_op jit(solution)/shard_map/pallas_call | solution.py:475
  40.2 0.3 shard_map.68.early
  40.5 0.0 collective-permute-done.4.refs_0_.refs_2_
  40.5 0.3 shard_map.69
  40.8 1.5 %collective-permute-start.6 = (f32[1,128]{1,0:T(1,128)S(1)}, f32[1,128]{1,0:T(1,128)S(1)}, u32[]{:S(2)}, u32[]{:S(2)}) collective-permute-start(f32[1,128]{1,0:T(1,128)S(1)} %shard_map.69), channel_id=1, source_target_pairs={{0,24},{4,28},{8,16},{12,20},{16,8},{20,12},{24,0},{28,4},{1,25},{... | collective-permute-start | bytes 1544 | tf_op jit(solution)/shard_map/ppermute | solution.py:402
  42.3 1.5 %collective-permute-start.7 = (f32[1,128]{1,0:T(1,128)S(1)}, f32[1,128]{1,0:T(1,128)S(1)}, u32[]{:S(2)}, u32[]{:S(2)}) collective-permute-start(f32[1,128]{1,0:T(1,128)S(1)} %shard_map.69), channel_id=1, source_target_pairs={{0,16},{4,20},{8,24},{12,28},{16,0},{20,4},{24,8},{28,12},{1,17},{... | collective-permute-start | bytes 1544 | tf_op jit(solution)/shard_map/ppermute | solution.py:402
  43.7 0.5 %collective-permute-start.8 = (f32[1,128]{1,0:T(1,128)S(1)}, f32[1,128]{1,0:T(1,128)S(1)}, u32[]{:S(2)}, u32[]{:S(2)}) collective-permute-start(f32[1,128]{1,0:T(1,128)S(1)} %shard_map.69), channel_id=1, source_target_pairs={{0,8},{4,12},{8,0},{12,4},{16,24},{20,28},{24,16},{28,20},{1,9},{5... | collective-permute-start | bytes 1544 | tf_op jit(solution)/shard_map/ppermute | solution.py:402
  44.3 1.0 %collective-permute-done.6 = f32[1,128]{1,0:T(1,128)S(1)} collective-permute-done((f32[1,128]{1,0:T(1,128)S(1)}, f32[1,128]{1,0:T(1,128)S(1)}, u32[]{:S(2)}, u32[]{:S(2)}) %collective-permute-start.6) | collective-permute-done | bytes 544 | tf_op jit(solution)/shard_map/ppermute | solution.py:402
  45.3 0.6 %collective-permute-done.7 = f32[1,128]{1,0:T(1,128)S(1)} collective-permute-done((f32[1,128]{1,0:T(1,128)S(1)}, f32[1,128]{1,0:T(1,128)S(1)}, u32[]{:S(2)}, u32[]{:S(2)}) %collective-permute-start.7) | collective-permute-done | bytes 544 | tf_op jit(solution)/shard_map/ppermute | solution.py:402
  45.8 1.5 %collective-permute-done.8 = f32[1,128]{1,0:T(1,128)S(1)} collective-permute-done((f32[1,128]{1,0:T(1,128)S(1)}, f32[1,128]{1,0:T(1,128)S(1)}, u32[]{:S(2)}, u32[]{:S(2)}) %collective-permute-start.8) | collective-permute-done | bytes 544 | tf_op jit(solution)/shard_map/ppermute | solution.py:402
  47.3 1.2 %collective-permute-done.9.refs_5_ = f32[1,128]{1,0:T(1,128)S(1)} collective-permute-done((f32[1,128]{1,0:T(1,128)S(1)}, f32[1,128]{1,0:T(1,128)S(1)}, u32[]{:S(2)}, u32[]{:S(2)}) %collective-permute-start.9) | collective-permute-done | bytes 544 | tf_op jit(solution)/shard_map/ppermute | solution.py:402
  48.5 1.1 %shard_map.70 = f32[2,8,64,128]{3,2,1,0:T(8,128)} custom-call(s32[1]{0:T(128)} %bitcast.outside, f32[2,8,64,128]{3,2,1,0:T(8,128)S(1)} %shard_map.67.update, f32[2,8,64,128]{3,2,1,0:T(8,128)S(1)} %copy-done.1, f32[2,8,64,128]{3,2,1,0:T(8,128)S(1)} %collective-permute-done.2.refs_0_, f32[2,8,64,128]{3,2,1,0:T(8,128)S(1)} %collective-permute-done.3.refs_1_, ...), custom_call_target="tpu_custom_call" | custom-call | tf_op jit(solution)/shard_map/pallas_call | solution.py:514
  (13 shorter events, 0.0 us)
Async XLA Ops:
  0.0 9.2 %copy-start = (f32[2,8,64,128]{3,2,1,0:T(8,128)S(1)}, f32[2,8,64,128]{3,2,1,0:T(8,128)}, u32[]{:S(2)}) copy-start(f32[2,8,64,128]{3,2,1,0:T(8,128)} %own.3) | copy-start | bytes 1572868
  0.0 16.7 %collective-permute-start.2 = (f32[2,8,64,128]{3,2,1,0:T(8,128)}, f32[2,8,64,128]{3,2,1,0:T(8,128)S(1)}, u32[]{:S(2)}, u32[]{:S(2)}) collective-permute-start(f32[2,8,64,128]{3,2,1,0:T(8,128)} %own.3), channel_id=1, source_target_pairs={{0,2},{3,1},{2,3},{1,0},{4,6},{7,5},{6,7},{5,4},{8,10},{11,9},{10,... | collective-permute-start | bytes 1572872 | tf_op jit(solution)/shard_map/ppermute | solution.py:377
  6.5 15.9 %collective-permute-start = (f32[11,64,128]{2,1,0:T(8,128)S(1)}, f32[11,64,128]{2,1,0:T(8,128)}, u32[]{:S(2)}, u32[]{:S(2)}) collective-permute-start(f32[11,64,128]{2,1,0:T(8,128)S(1)} %get-tuple-element.15.up), channel_id=1, source_target_pairs={{0,4},{4,8},{8,12},{12,16},{16,20},{20,24},{24,28},{28,0},{1,5},{5... | collective-permute-start | bytes 1081352 | tf_op jit(solution)/shard_map/ppermute | solution.py:451
  6.5 15.9 %copy-start.3 = (f32[8,64,128]{2,1,0:T(8,128)S(1)}, f32[8,64,128]{2,1,0:T(8,128)}, u32[]{:S(2)}) copy-start(f32[8,64,128]{2,1,0:T(8,128)} %potential.1) | copy-start | bytes 786436
  6.5 15.8 %collective-permute-start.1 = (f32[11,64,128]{2,1,0:T(8,128)}, f32[11,64,128]{2,1,0:T(8,128)}, u32[]{:S(2)}, u32[]{:S(2)}) collective-permute-start(f32[11,64,128]{2,1,0:T(8,128)} %get-tuple-element.16.down), channel_id=1, source_target_pairs={{4,0},{8,4},{12,8},{16,12},{20,16},{24,20},{28,24},{0,28},{5,1},{9... | collective-permute-start | bytes 1081352 | tf_op jit(solution)/shard_map/ppermute | solution.py:452
  9.2 31.0 %collective-permute-start.3 = (f32[2,8,64,128]{3,2,1,0:T(8,128)S(1)}, f32[2,8,64,128]{3,2,1,0:T(8,128)S(1)}, u32[]{:S(2)}, u32[]{:S(2)}) collective-permute-start(f32[2,8,64,128]{3,2,1,0:T(8,128)S(1)} %copy-done), channel_id=1, source_target_pairs={{1,3},{2,0},{0,1},{3,2},{5,7},{6,4},{4,5},{7,6},{9,11},{10,8},{8,9... | collective-permute-start | bytes 1572872 | tf_op jit(solution)/shard_map/ppermute | solution.py:378
  9.2 31.3 %collective-permute-start.4 = (f32[2,8,64,128]{3,2,1,0:T(8,128)S(1)}, f32[2,8,64,128]{3,2,1,0:T(8,128)S(1)}, u32[]{:S(2)}, u32[]{:S(2)}) collective-permute-start(f32[2,8,64,128]{3,2,1,0:T(8,128)S(1)} %copy-done), channel_id=1, source_target_pairs={{1,2},{2,1},{0,0},{3,3},{5,6},{6,5},{4,4},{7,7},{9,10},{10,9},{8,8... | collective-permute-start | bytes 1572872 | tf_op jit(solution)/shard_map/ppermute | solution.py:379
  16.7 23.8 %collective-permute-start.5 = (f32[2,8,64,128]{3,2,1,0:T(8,128)S(1)}, f32[2,8,64,128]{3,2,1,0:T(8,128)S(1)}, u32[]{:S(2)}, u32[]{:S(2)}) collective-permute-start(f32[2,8,64,128]{3,2,1,0:T(8,128)S(1)} %collective-permute-done.2.refs_0_), channel_id=1, source_target_pairs={{2,3},{1,0},{0,1},{3,2},{6,7},{5,4},{4,5},{7,6},{10,11},{9,8},{8,9... | collective-permute-start | bytes 1572872 | tf_op jit(solution)/shard_map/ppermute | solution.py:380
  20.8 0.8 %copy-start.4 = (f32[2,8,64,128]{3,2,1,0:T(8,128)}, f32[2,8,64,128]{3,2,1,0:T(8,128)S(1)}, u32[]{:S(2)}) copy-start(f32[2,8,64,128]{3,2,1,0:T(8,128)S(1)} %get-tuple-element.13.own_scaled) | copy-start | bytes 1572868
  21.6 0.8 %copy-start.5 = (f32[2,8,64,128]{3,2,1,0:T(8,128)}, f32[2,8,64,128]{3,2,1,0:T(8,128)S(1)}, u32[]{:S(2)}) copy-start(f32[2,8,64,128]{3,2,1,0:T(8,128)S(1)} %get-tuple-element.14.own_weight) | copy-start | bytes 1572868
  22.4 0.7 %copy-start.6 = (f32[8]{0:T(128)S(1)}, f32[8]{0:T(128)}, u32[]{:S(2)}) copy-start(f32[8]{0:T(128)} %shifts.3) | copy-start | bytes 100
  22.4 0.7 %copy-start.7 = (s32[2]{0:T(128)S(1)}, s32[2]{0:T(128)}, u32[]{:S(2)}) copy-start(s32[2]{0:T(128)} %assigned.3) | copy-start | bytes 28
  25.8 10.6 %copy-start.2 = (f32[2,8,64,128]{3,2,1,0:T(8,128)S(1)}, f32[2,8,64,128]{3,2,1,0:T(8,128)}, u32[]{:S(2)}) copy-start(f32[2,8,64,128]{3,2,1,0:T(8,128)} %guess.1) | copy-start | bytes 1572868
  36.3 3.9 %copy-start.1 = (f32[2,8,64,128]{3,2,1,0:T(8,128)S(1)}, f32[2,8,64,128]{3,2,1,0:T(8,128)}, u32[]{:S(2)}) copy-start(f32[2,8,64,128]{3,2,1,0:T(8,128)} %own.3) | copy-start | bytes 1572868
  40.8 4.5 %collective-permute-start.6 = (f32[1,128]{1,0:T(1,128)S(1)}, f32[1,128]{1,0:T(1,128)S(1)}, u32[]{:S(2)}, u32[]{:S(2)}) collective-permute-start(f32[1,128]{1,0:T(1,128)S(1)} %shard_map.69), channel_id=1, source_target_pairs={{0,24},{4,28},{8,16},{12,20},{16,8},{20,12},{24,0},{28,4},{1,25},{... | collective-permute-start | bytes 1544 | tf_op jit(solution)/shard_map/ppermute | solution.py:402
  42.3 3.6 %collective-permute-start.7 = (f32[1,128]{1,0:T(1,128)S(1)}, f32[1,128]{1,0:T(1,128)S(1)}, u32[]{:S(2)}, u32[]{:S(2)}) collective-permute-start(f32[1,128]{1,0:T(1,128)S(1)} %shard_map.69), channel_id=1, source_target_pairs={{0,16},{4,20},{8,24},{12,28},{16,0},{20,4},{24,8},{28,12},{1,17},{... | collective-permute-start | bytes 1544 | tf_op jit(solution)/shard_map/ppermute | solution.py:402
  43.7 3.6 %collective-permute-start.8 = (f32[1,128]{1,0:T(1,128)S(1)}, f32[1,128]{1,0:T(1,128)S(1)}, u32[]{:S(2)}, u32[]{:S(2)}) collective-permute-start(f32[1,128]{1,0:T(1,128)S(1)} %shard_map.69), channel_id=1, source_target_pairs={{0,8},{4,12},{8,0},{12,4},{16,24},{20,28},{24,16},{28,20},{1,9},{5... | collective-permute-start | bytes 1544 | tf_op jit(solution)/shard_map/ppermute | solution.py:402
  47.3 1.2 %collective-permute-start.9 = (f32[1,128]{1,0:T(1,128)S(1)}, f32[1,128]{1,0:T(1,128)S(1)}, u32[]{:S(2)}, u32[]{:S(2)}) collective-permute-start(f32[1,128]{1,0:T(1,128)S(1)} %add_add_fusion.refs_4_), channel_id=1, source_target_pairs={{0,4},{4,0},{8,12},{12,8},{16,20},{20,16},{24,28},{28,24},{1,5},{5... | collective-permute-start | bytes 1544 | tf_op jit(solution)/shard_map/ppermute | solution.py:402
